TPU v7x, 128 devices: a whole 4x4x4 slice. The times are simulated.
128 devices in a mesh: train: 8 (over z, x_hi), serve: 16 (over x_lo, y, core).
Axes of the slice: x: 4 (x_hi: 2, x_lo: 2; x = x_hi * 2 + x_lo), y: 4, z: 4, core: 2. Of those that a mesh axis runs over, the one named last changes fastest.
Arguments:
- train_weights: bfloat16 [16, 7680, 2112], P(None, 'train', 'serve'), may hold values from -6 to 6
- row_offset: int32 [16, 9], replicated, may hold values from 0 to 7168, as said below
- block_group: int32 [16, 224, 1], P(None, 'train'), may hold values from 0 to 15; in each aligned block of 28 rows (0 to 27, 28 to 55, ..., all dimensions but the last counted through in order) at most 3 rows name the same one
Outputs:
- quant_codes: bfloat16 [16, 16, 8, 3, 32, 2112], P(None, 'serve', 'train')
- block_scales: float32 [16, 16, 8, 3, 2112], P(None, 'serve', 'train')
Inputs may be any that keep to these rules, and one draw needn't show every extreme that they name: For every layer l: row_offset[l, 0] = 0 and row_offset[l, 8] = 7168; every other row_offset[l, t] lies 1 to 32 rows above or below t * 896, never on it; in every layer one entry lies exactly 32 rows above and another exactly 32 rows below; layer 1 has the opposite sign of layer 0 at every such entry. `block_group`: within each aligned block of 28 entries (one training device's blocks of one layer), no group is named more than 3 times; some group reaches 3 in some of them.
All inputs are finite; a program needn't handle non-finite values.
Results may differ from a plain program's by a relative error of at most 0.001.
Values may be sent and summed in bfloat16 or wider, within the bound.
No kernel may reach another device: no remote copies, remote signals or barrier semaphores. Data moves between devices by JAX's collectives and lax.ppermute only.
A program may use at most 128 MiB of HBM per device.

v0:
```python
import jax
import jax.numpy as jnp
from jax import lax
from jax.experimental import pallas as pl
from jax.experimental.pallas import tpu as pltpu
from jax.sharding import Mesh
from jax.sharding import PartitionSpec as P


BLOCK = 32
SHIFT = 32
LANES = 128
PACK = 16
SERVE = ("x", "y", "core")
SIDES = (2, 4, 2)
OFFSETS = [
    (dx, dy, dc)
    for dx, dy in ((1, 2), (0, 1), (1, 1), (0, 3), (0, 2), (1, 3), (1, 0), (0, 0))
    for dc in (1, 0)
]
LATER = sorted(range(len(OFFSETS)), key=lambda p: (-OFFSETS[p][0], p))
FIRST, SECOND, THIRD = 28, 12, 20
ENTRIES = 64
NT = (((1,), (1,)), ((), ()))
F32 = jnp.float32
BF16 = jnp.bfloat16
MIB = 1024 * 1024


def iota(shape, dim):
    return lax.broadcasted_iota(jnp.int32, shape, dim)


def identity(n):
    return (iota((n, n), 0) == iota((n, n), 1)).astype(BF16)


def layer_major():
    out, src = iota((PACK * PACK, PACK * PACK), 0), iota((PACK * PACK, PACK * PACK), 1)
    return ((out // PACK == src % PACK) & (out % PACK == src // PACK)).astype(BF16)


def rest_major():
    out, src = iota((LANES, 4 * PACK), 0), iota((LANES, 4 * PACK), 1)
    return ((out // 4 == src % PACK) & (out % 4 == src // PACK)).astype(BF16)


def dot(a, b):
    return jnp.dot(a, b, preferred_element_type=F32)


def turn(eye, value):
    return lax.dot_general(eye, value, NT, preferred_element_type=F32)


def ahead(me, offset):
    dx, dy, dc = offset
    return (me ^ (8 * dx + dc)) & 9 | ((me >> 1) + dy & 3) << 1


def behind(me, offset):
    dx, dy, dc = offset
    return ahead(me, (dx, -dy & 3, dc))


def fill(refs, me, group, start, size, end, block, ref):
    table_ref, extra_ref = refs
    lane_group = iota((BLOCK, LANES), 1) >> 2
    rest = jnp.zeros((BLOCK, LANES), F32)
    for n in range(size):
        j = start + n
        entry = jnp.where(j < end, table_ref[group * ENTRIES + j], SHIFT)
        layer, at = entry >> 10, pl.multiple_of(entry & 1023, BLOCK)
        ref[n] = block(layer, at)
        place = j + me & 31
        moved = pltpu.roll(extra_ref[pl.ds(at, BLOCK), :], 4 * (place - layer) & (LANES - 1), 1)
        rest = jnp.where(lane_group == place, moved, rest)
    ref[size] = rest.astype(BF16)


def turn_kernel(me_ref, group_ref, x_hbm, *refs):
    peers = len(OFFSETS)
    first_set, (rows_hbm, extra_ref, head_ref, tail_ref, table_ref, inner_ref, end_ref) = refs[:peers], refs[peers : peers + 7]
    x_ref, planes, rows_ref, sems, out_sem = refs[peers + 7 :]
    length = x_ref.shape[2]
    steps = LANES // PACK
    spare = PACK - 4
    parts = [(LANES - spare, spare, 0)] + [(PACK * i, PACK, spare + PACK * i) for i in range(steps)]
    parts.append((LANES, 4, spare + LANES))
    copies = [
        pltpu.make_async_copy(x_hbm.at[pl.ds(src, n)], x_ref.at[pl.ds(dst, n)], sems.at[i])
        for i, (src, n, dst) in enumerate(parts)
    ]
    for copy in copies:
        copy.start()
    layers, blocks = group_ref.shape
    groups = inner_ref.shape[0]

    def enter(count_ref, layer, b):
        group = group_ref[layer, b]
        j = count_ref[group]
        count_ref[group] = j + 1
        table_ref[group * ENTRIES + j] = (layer << 10) + SHIFT + BLOCK * b

    for g in range(groups):
        inner_ref[g] = 0
    perm = layer_major()
    me = me_ref[0]
    turns, part = me >> 2, 4 * (me & 3)
    copies[0].wait()
    for i in range(steps):
        copies[i + 1].wait()
        x = x_ref[pl.ds(spare + PACK * i - part, PACK)].reshape(PACK * PACK, length)
        at = pl.multiple_of(PACK * ((i + turns) & (steps - 1)), PACK)
        planes[:, pl.ds(at, PACK), :] = dot(perm, x).astype(BF16).reshape(PACK, PACK, length)
        for layer in range(layers * i // steps, layers * (i + 1) // steps):
            for b in range(1, blocks - 1):
                enter(inner_ref, layer, b)
    copies[steps + 1].wait()
    rest = dot(rest_major(), x_ref[pl.ds(spare + LANES, 4)].reshape(4 * PACK, length)).astype(BF16)
    for start in range(0, length, 256):
        size = min(256, length - start)
        extra_ref[start : start + size, :] = turn(identity(size), rest[:, start : start + size])
    for g in range(groups):
        end_ref[g] = jnp.maximum(inner_ref[g], FIRST)
    for layer in range(layers):
        for b in (0, blocks - 1):
            enter(end_ref, layer, b)

    def layer_step(layer, carry):
        turned = jnp.transpose(planes[layer])
        rows_ref[layer] = turned
        head_ref[layer] = turned[:SHIFT]
        tail_ref[layer] = turned[length - SHIFT :]
        pltpu.make_async_copy(rows_ref.at[layer], rows_hbm.at[layer], out_sem).start()
        return carry

    lax.fori_loop(0, layers, layer_step, 0)
    head_ref[layers] = extra_ref[:SHIFT].astype(BF16)
    tail_ref[layers] = extra_ref[length - SHIFT :].astype(BF16)
    for p, offset in enumerate(OFFSETS):
        group = ahead(me, offset)
        fill(
            (table_ref, extra_ref), me, group, 0, FIRST, inner_ref[group],
            lambda layer, at: rows_ref[layer, pl.ds(at, BLOCK), :], first_set[p],
        )
    pltpu.make_async_copy(rows_ref, rows_hbm, out_sem).wait()


def rest_kernel(me_ref, shard_ref, offset_ref, table_ref, end_ref, rows_hbm, rest_ref, left_ref, right_ref, *refs):
    peers = len(OFFSETS)
    second_set, third_ref, (rows_ref, edge_ref, extra_ref, sem) = refs[:peers], refs[peers], refs[peers + 1 :]
    load = pltpu.make_async_copy(rows_hbm, rows_ref, sem)
    load.start()
    load.wait()
    layers, length = rows_ref.shape[:2]
    row = iota((BLOCK, LANES), 0)
    lane_group = iota((BLOCK, LANES), 1) >> 2
    me, shard = me_ref[0], shard_ref[0]
    last = length - 2 * SHIFT
    before = shard * (length - 2 * SHIFT)

    def edge_step(layer, carry):
        first, after = carry
        start = offset_ref[layer, shard] - before
        end = offset_ref[layer, shard + 1] - before - (last - SHIFT)
        edge_ref[layer, :SHIFT] = jnp.where(row < start, left_ref[layer], rows_ref[layer, SHIFT : 2 * SHIFT])
        edge_ref[layer, SHIFT:] = jnp.where(row >= end, right_ref[layer], rows_ref[layer, last : last + SHIFT])
        return jnp.where(lane_group == layer, start, first), jnp.where(lane_group == layer, end, after)

    nothing = jnp.zeros((BLOCK, LANES), jnp.int32)
    first, after = lax.fori_loop(0, layers, edge_step, (nothing, nothing), unroll=4)
    extra_ref[...] = rest_ref[...]
    extra_ref[SHIFT : 2 * SHIFT] = jnp.where(row < first, left_ref[layers].astype(F32), rest_ref[SHIFT : 2 * SHIFT])
    extra_ref[last : last + SHIFT] = jnp.where(row >= after, right_ref[layers].astype(F32), rest_ref[last : last + SHIFT])

    def block(layer, at):
        low, high = at == SHIFT, at == last
        edge = edge_ref[layer, pl.ds(pl.multiple_of(jnp.where(high, SHIFT, 0), BLOCK), BLOCK), :]
        return jnp.where(low | high, edge, rows_ref[layer, pl.ds(at, BLOCK), :])

    for p, offset in enumerate(OFFSETS):
        group = ahead(me, offset)
        fill((table_ref, extra_ref), me, group, FIRST, SECOND, end_ref[group], block, second_set[p])

    def third_step(group, carry):
        @pl.when(end_ref[group] > FIRST + SECOND)
        def _():
            fill((table_ref, extra_ref), me, group, FIRST + SECOND, THIRD, end_ref[group], block, third_ref.at[group])

        return carry

    lax.fori_loop(0, peers, third_step, 0)


def join_slot(held, n, tile, jj, code_ref, scale_ref, width):
    peers = held.shape[0]
    lane = iota((BLOCK, LANES), 1)
    source = (lane >> 2) - jj & 31
    rest = jnp.zeros((BLOCK, LANES), F32)
    for s in range(peers):
        rest = jnp.where(source == s, held[s, tile].astype(F32), rest)
    rest = pltpu.roll(rest, -4 * jj & (LANES - 1), 1)
    before = None
    for t in range(peers + 1):
        x = rest
        if before is not None:
            x = jnp.where(lane < 4 * t - 4, before, x)
        if t < peers:
            own = held[t, n].astype(F32)
            x = own if t == 0 else jnp.where(lane >= 4 * t, own, x)
            before = own
        size = min(LANES, width - LANES * t)
        top = jnp.maximum(jnp.max(jnp.abs(x), axis=0, keepdims=True), 0.25)
        scale_ref[:, LANES * t : LANES * t + size] = top[:, :size]
        code_ref[:, LANES * t : LANES * t + size] = (x * (1.0 / top)).astype(BF16)[:, :size]


def write_slots(slot_ref, used_ref, codes_hbm, scale_hbm, code_ref, scale_ref, code_sem, scale_sem, low, high, compute):
    layers = used_ref.shape[0]
    per_layer = codes_hbm.shape[0] // layers
    ring = code_ref.shape[0]

    def stores(i, slot):
        return (
            pltpu.make_async_copy(code_ref.at[i], codes_hbm.at[slot], code_sem.at[i]),
            pltpu.make_async_copy(scale_ref.at[i], scale_hbm.at[slot], scale_sem.at[i]),
        )

    def layer_step(layer, done):
        for k in range(per_layer):
            j = slot_ref[per_layer * layer + k]
            mine = (k < used_ref[layer]) & (j >= low) & (j < high)
            i = done & (ring - 1)

            @pl.when(mine)
            def _(j=j, i=i, done=done, k=k):
                @pl.when(done >= ring)
                def _():
                    for store in stores(i, 0):
                        store.wait()

                compute(j, code_ref.at[i], scale_ref.at[i])
                for store in stores(i, per_layer * layer + k):
                    store.start()

            done = done + mine.astype(jnp.int32)
        return done

    done = lax.fori_loop(0, layers, layer_step, jnp.int32(0))
    for i in range(ring):

        @pl.when(done > i)
        def _(i=i):
            for store in stores(i, 0):
                store.wait()


def join_first_kernel(me_ref, group_ref, inner_ref, *refs):
    peers = len(OFFSETS)
    parts, (codes_hbm, scale_hbm, slot_ref, used_ref) = refs[:peers], refs[peers : peers + 4]
    held, code_ref, scale_ref, zero_code, zero_scale, sems, code_sem, scale_sem, zero_sem = refs[peers + 4 :]
    me, width = me_ref[0], codes_hbm.shape[2]
    layers, blocks = group_ref.shape
    per_layer = codes_hbm.shape[0] // layers
    loads = [pltpu.make_async_copy(part, held.at[behind(me, o)], sems.at[p]) for p, (part, o) in enumerate(zip(parts, OFFSETS))]
    for load in loads:
        load.start()
    zero_code[...] = jnp.zeros_like(zero_code)
    zero_scale[...] = jnp.zeros_like(zero_scale)

    def find(layer, carry):
        inner, edge = carry
        k = jnp.int32(0)
        for b in range(blocks):
            mine = (group_ref[layer, b] == me).astype(jnp.int32)
            at_edge = b in (0, blocks - 1)
            slot_ref[jnp.where(mine == 1, per_layer * layer + k, per_layer * layers)] = edge if at_edge else inner
            k = k + mine
            inner, edge = (inner, edge + mine) if at_edge else (inner + mine, edge)
        used_ref[layer] = k
        return inner, edge

    lax.fori_loop(0, layers, find, (jnp.int32(0), jnp.maximum(inner_ref[me], FIRST)))

    def clear(slot):
        return (
            pltpu.make_async_copy(zero_code, codes_hbm.at[slot], zero_sem.at[0]),
            pltpu.make_async_copy(zero_scale, scale_hbm.at[slot], zero_sem.at[1]),
        )

    def each_empty(act):
        def layer_step(layer, carry):
            for k in range(per_layer):

                @pl.when(k >= used_ref[layer])
                def _(k=k):
                    for copy in clear(per_layer * layer + k):
                        act(copy)

            return carry

        lax.fori_loop(0, layers, layer_step, 0)

    each_empty(lambda copy: copy.start())
    for load in loads:
        load.wait()

    def compute(j, code, scale):
        join_slot(held, j, FIRST, j, code, scale, width)

    write_slots(slot_ref, used_ref, codes_hbm, scale_hbm, code_ref, scale_ref, code_sem, scale_sem, 0, FIRST, compute)
    each_empty(lambda copy: copy.wait())


def join_last_kernel(me_ref, slot_ref, used_ref, end_ref, *refs):
    peers = len(OFFSETS)
    parts, third_hbm, (codes_hbm, scale_hbm) = refs[:peers], refs[peers], refs[peers + 3 : peers + 5]
    held, code_ref, scale_ref, sems, code_sem, scale_sem = refs[peers + 5 :]
    me, width = me_ref[0], codes_hbm.shape[2]
    loads = [
        pltpu.make_async_copy(part, held.at[behind(me, o), pl.ds(0, SECOND + 1)], sems.at[p])
        for p, (part, o) in enumerate(zip(parts, OFFSETS))
    ]
    for load in loads:
        load.start()

    @pl.when(end_ref[me] > FIRST + SECOND)
    def _():
        load = pltpu.make_async_copy(third_hbm, held.at[:, pl.ds(SECOND + 1, THIRD + 1)], sems.at[peers])
        load.start()
        load.wait()

    for load in loads:
        load.wait()

    def compute(j, code, scale):
        late = (j >= FIRST + SECOND).astype(jnp.int32)
        join_slot(held, j - FIRST + late, SECOND + late * (THIRD + 1), j & 31, code, scale, width)

    write_slots(
        slot_ref, used_ref, codes_hbm, scale_hbm, code_ref, scale_ref, code_sem, scale_sem, FIRST, ENTRIES, compute
    )


def in_vmem():
    return pl.BlockSpec(memory_space=pltpu.VMEM)


def in_hbm():
    return pl.BlockSpec(memory_space=pltpu.HBM)


def anywhere():
    return pl.BlockSpec(memory_space=pl.ANY)


def hbm(value):
    return pltpu.with_memory_space_constraint(value, pltpu.HBM)


def in_smem():
    return pl.BlockSpec(memory_space=pltpu.SMEM)


def sent_to(value, offset):
    count = SIDES[0] * SIDES[1] * SIDES[2]
    return lax.ppermute(value, SERVE, [(i, ahead(i, offset)) for i in range(count)])


def shards(train_weights, row_offset, block_group):
    train_n = lax.axis_size("train")
    serve_n = lax.axis_size(SERVE)
    train_idx = lax.axis_index("train")
    serve_idx = lax.axis_index(SERVE).astype(jnp.int32)
    layers, buffer_len, columns = train_weights.shape
    blocks_dev = block_group.shape[1]
    per_layer = (blocks_dev + serve_n - 1) // serve_n + 1
    slots = layers * per_layer
    width = columns * serve_n
    groups = block_group[:, :, 0]
    me, shard = serve_idx.reshape(1), train_idx.astype(jnp.int32).reshape(1)
    by_column = hbm(jnp.transpose(train_weights, (2, 0, 1)))

    peers = len(OFFSETS)
    steps = LANES // PACK
    edge = jax.ShapeDtypeStruct((layers + 1, SHIFT, LANES), BF16)
    per_group = jax.ShapeDtypeStruct((serve_n,), jnp.int32)
    turned = pl.pallas_call(
        turn_kernel,
        in_specs=[in_smem(), in_smem(), in_hbm()],
        out_specs=[in_vmem()] * peers + [in_hbm()] + [in_vmem()] * 3 + [in_smem()] * 3,
        out_shape=[jax.ShapeDtypeStruct((FIRST + 1, BLOCK, LANES), BF16)] * peers
        + [
            pltpu.HBM((layers, buffer_len, LANES), BF16),
            jax.ShapeDtypeStruct((buffer_len, LANES), F32),
            edge,
            edge,
            jax.ShapeDtypeStruct((serve_n * ENTRIES,), jnp.int32),
            per_group,
            per_group,
        ],
        scratch_shapes=[
            pltpu.VMEM((columns + PACK - 4, layers, buffer_len), BF16),
            pltpu.VMEM((layers, LANES, buffer_len), BF16),
            pltpu.VMEM((layers, buffer_len, LANES), BF16),
            pltpu.SemaphoreType.DMA((steps + 2,)),
            pltpu.SemaphoreType.DMA,
        ],
        compiler_params=pltpu.CompilerParams(vmem_limit_bytes=24 * MIB),
        cost_estimate=pl.CostEstimate(flops=3 * 10**9, bytes_accessed=9 * 10**6, transcendentals=0),
        name="turn",
    )(me, groups, by_column)
    first_sent, (rows, rest, head, tail, table, inner, end) = turned[:peers], turned[peers:]
    left = lax.ppermute(tail, "train", [(i, i + 1) for i in range(train_n - 1)])
    right = lax.ppermute(head, "train", [(i + 1, i) for i in range(train_n - 1)])
    *second_sent, third_sent = pl.pallas_call(
        rest_kernel,
        in_specs=[in_smem()] * 5 + [in_hbm()] + [in_vmem()] * 3,
        out_specs=[in_vmem()] * (peers + 1),
        out_shape=[jax.ShapeDtypeStruct((SECOND + 1, BLOCK, LANES), BF16)] * peers
        + [jax.ShapeDtypeStruct((serve_n, THIRD + 1, BLOCK, LANES), BF16)],
        scratch_shapes=[
            pltpu.VMEM((layers, buffer_len, LANES), BF16),
            pltpu.VMEM((layers, 2 * SHIFT, LANES), BF16),
            pltpu.VMEM((buffer_len, LANES), F32),
            pltpu.SemaphoreType.DMA,
        ],
        compiler_params=pltpu.CompilerParams(vmem_limit_bytes=16 * MIB),
        cost_estimate=pl.CostEstimate(flops=10**9, bytes_accessed=10**7, transcendentals=0),
        name="rest",
    )(me, shard, row_offset, table, end, hbm(rows), rest, left, right)

    got_first = [sent_to(v, o) for v, o in zip(first_sent[:-1], OFFSETS)] + [first_sent[-1]]
    got_second = list(second_sent)
    for p in LATER:
        if p < peers - 1:
            got_second[p] = sent_to(second_sent[p], OFFSETS[p])
    got_third = lax.cond(
        jnp.max(end) > FIRST + SECOND,
        lambda v: lax.all_to_all(v, SERVE, split_axis=0, concat_axis=0, tiled=True),
        lambda v: v,
        third_sent,
    )
    ring = 4
    results = [pltpu.HBM((slots, BLOCK, width), BF16), pltpu.HBM((slots, 1, width), F32)]
    buffers = [pltpu.VMEM((ring, BLOCK, width), BF16), pltpu.VMEM((ring, 1, width), F32)]
    codes, scales, slot_of, used = pl.pallas_call(
        join_first_kernel,
        in_specs=[in_smem()] * 3 + [anywhere()] * peers,
        out_specs=[in_hbm(), in_hbm(), in_smem(), in_smem()],
        out_shape=results
        + [jax.ShapeDtypeStruct((slots + 1,), jnp.int32), jax.ShapeDtypeStruct((layers,), jnp.int32)],
        scratch_shapes=[
            pltpu.VMEM((serve_n, FIRST + 1, BLOCK, LANES), BF16),
            *buffers,
            pltpu.VMEM((BLOCK, width), BF16),
            pltpu.VMEM((1, width), F32),
            pltpu.SemaphoreType.DMA((peers,)),
            pltpu.SemaphoreType.DMA((ring,)),
            pltpu.SemaphoreType.DMA((ring,)),
            pltpu.SemaphoreType.DMA((2,)),
        ],
        compiler_params=pltpu.CompilerParams(vmem_limit_bytes=16 * MIB),
        cost_estimate=pl.CostEstimate(flops=4 * 10**9, bytes_accessed=10**7, transcendentals=0),
        name="join_first",
    )(me, groups, inner, *got_first)
    codes, scales = pl.pallas_call(
        join_last_kernel,
        in_specs=[in_smem()] * 4 + [anywhere()] * (peers + 1) + [in_hbm()] * 2,
        out_specs=[in_hbm(), in_hbm()],
        out_shape=results,
        input_output_aliases={peers + 5: 0, peers + 6: 1},
        scratch_shapes=[
            pltpu.VMEM((serve_n, SECOND + THIRD + 2, BLOCK, LANES), BF16),
            *buffers,
            pltpu.SemaphoreType.DMA((peers + 1,)),
            pltpu.SemaphoreType.DMA((ring,)),
            pltpu.SemaphoreType.DMA((ring,)),
        ],
        compiler_params=pltpu.CompilerParams(vmem_limit_bytes=16 * MIB),
        cost_estimate=pl.CostEstimate(flops=10**9, bytes_accessed=10**7, transcendentals=0),
        name="join_last",
    )(me, slot_of, used, end, *got_second, got_third, codes, scales)
    return (
        codes.reshape(layers, 1, 1, per_layer, BLOCK, width),
        scales.reshape(layers, 1, 1, per_layer, width),
    )


def solution(mesh):
    finer = Mesh(mesh.devices.reshape(mesh.shape["train"], *SIDES), ("train", *SERVE))

    return jax.shard_map(
        shards,
        mesh=finer,
        in_specs=(P(None, "train", SERVE), P(), P(None, "train", None)),
        out_specs=(P(None, SERVE, "train", None, None, None), P(None, SERVE, "train", None, None)),
        check_vma=False,
    )
```

profile of v0, /device:TPU:43, one launch (start us, length us, event | category | flops | bytes accessed | tf_op | source)
XLA Modules:
  0.0 142.1 jit_solution(18156667127516894315)
XLA Ops:
  1.3 10.0 %turn.1 = (bf16[29,32,128]{2,1,0:T(8,128)(2,1)S(1)}, bf16[29,32,128]{2,1,0:T(8,128)(2,1)S(1)}, bf16[29,32,128]{2,1,0:T(8,128)(2,1)S(1)}, bf16[29,32,128]{2,1,0:T...) custom-call(s32[1]{0:T(128)} %bitcast.me_ref, ...), custom_call_target="tpu_custom_call" | custom-call | flops 3000000000 | bytes 9000000 | tf_op jit(solution)/shard_map/turn/pallas_call | solution.py:389
  12.0 3.7 %collective-permute-start.15 = (bf16[17,32,128]{2,1,0:T(8,128)(2,1)S(1)}, bf16[17,32,128]{2,1,0:T(8,128)(2,1)S(1)}, u32[]{:S(2)}, u32[]{:S(2)}) collective-permute-start(bf16[17,32,128]{2,1,0:T(8,128)(2,1)S(1)} %get-tuple-element.76), channel_id=1, source_target_pairs={{0,16},{16,32},{32,48},{48,64},{64,80},{80,96},{96,112},{1,17},{17... | collective-permute-start | bytes 417800 | tf_op jit(solution)/shard_map/ppermute | solution.py:415
  15.8 3.9 %collective-permute-start.16 = (bf16[17,32,128]{2,1,0:T(8,128)(2,1)S(1)}, bf16[17,32,128]{2,1,0:T(8,128)(2,1)S(1)}, u32[]{:S(2)}, u32[]{:S(2)}) collective-permute-start(bf16[17,32,128]{2,1,0:T(8,128)(2,1)S(1)} %get-tuple-element.77), channel_id=1, source_target_pairs={{16,0},{32,16},{48,32},{64,48},{80,64},{96,80},{112,96},{17,1},{33... | collective-permute-start | bytes 417800 | tf_op jit(solution)/shard_map/ppermute | solution.py:416
  19.7 3.2 %collective-permute-start = (bf16[29,32,128]{2,1,0:T(8,128)(2,1)S(1)}, bf16[29,32,128]{2,1,0:T(8,128)(2,1)S(1)}, u32[]{:S(2)}, u32[]{:S(2)}) collective-permute-start(bf16[29,32,128]{2,1,0:T(8,128)(2,1)S(1)} %get-tuple-element.54), channel_id=1, source_target_pairs={{0,13},{1,12},{2,15},{3,14},{4,9},{5,8},{6,11},{7,10},{8,5},{9,4},... | collective-permute-start | bytes 712712 | tf_op jit(solution)/shard_map/ppermute | solution.py:368
  22.9 1.9 %collective-permute-start.1 = (bf16[29,32,128]{2,1,0:T(8,128)(2,1)S(1)}, bf16[29,32,128]{2,1,0:T(8,128)(2,1)S(1)}, u32[]{:S(2)}, u32[]{:S(2)}) collective-permute-start(bf16[29,32,128]{2,1,0:T(8,128)(2,1)S(1)} %get-tuple-element.55), channel_id=1, source_target_pairs={{0,12},{1,13},{2,14},{3,15},{4,8},{5,9},{6,10},{7,11},{8,4},{9,5},... | collective-permute-start | bytes 712712 | tf_op jit(solution)/shard_map/ppermute | solution.py:368
  26.5 1.8 %collective-permute-start.4 = (bf16[29,32,128]{2,1,0:T(8,128)(2,1)S(1)}, bf16[29,32,128]{2,1,0:T(8,128)(2,1)S(1)}, u32[]{:S(2)}, u32[]{:S(2)}) collective-permute-start(bf16[29,32,128]{2,1,0:T(8,128)(2,1)S(1)} %get-tuple-element.58), channel_id=1, source_target_pairs={{0,11},{1,10},{2,13},{3,12},{4,15},{5,14},{6,9},{7,8},{8,3},{9,2},... | collective-permute-start | bytes 712712 | tf_op jit(solution)/shard_map/ppermute | solution.py:368
  28.4 2.5 %collective-permute-done.refs_0_ = bf16[29,32,128]{2,1,0:T(8,128)(2,1)S(1)} collective-permute-done((bf16[29,32,128]{2,1,0:T(8,128)(2,1)S(1)}, bf16[29,32,128]{2,1,0:T(8,128)(2,1)S(1)}, u32[]{:S(2)}, u32[]{:S(2)}) %collective-permute-start) | collective-permute-done | bytes 237600 | tf_op jit(solution)/shard_map/ppermute | solution.py:368
  31.3 4.6 %collective-permute-done.1.refs_1_ = bf16[29,32,128]{2,1,0:T(8,128)(2,1)S(1)} collective-permute-done((bf16[29,32,128]{2,1,0:T(8,128)(2,1)S(1)}, bf16[29,32,128]{2,1,0:T(8,128)(2,1)S(1)}, u32[]{:S(2)}, u32[]{:S(2)}) %collective-permute-start.1) | collective-permute-done | bytes 237600 | tf_op jit(solution)/shard_map/ppermute | solution.py:368
  36.0 2.8 %collective-permute-start.6 = (bf16[29,32,128]{2,1,0:T(8,128)(2,1)S(1)}, bf16[29,32,128]{2,1,0:T(8,128)(2,1)S(1)}, u32[]{:S(2)}, u32[]{:S(2)}) collective-permute-start(bf16[29,32,128]{2,1,0:T(8,128)(2,1)S(1)} %get-tuple-element.60), channel_id=1, source_target_pairs={{0,7},{1,6},{2,1},{3,0},{4,3},{5,2},{6,5},{7,4},{8,15},{9,14},{10,... | collective-permute-start | bytes 712712 | tf_op jit(solution)/shard_map/ppermute | solution.py:368
  38.8 12.2 %collective-permute-done.2.refs_2_ = bf16[29,32,128]{2,1,0:T(8,128)(2,1)S(1)} collective-permute-done((bf16[29,32,128]{2,1,0:T(8,128)(2,1)S(1)}, bf16[29,32,128]{2,1,0:T(8,128)(2,1)S(1)}, u32[]{:S(2)}, u32[]{:S(2)}) %collective-permute-start.2) | collective-permute-done | bytes 237600 | tf_op jit(solution)/shard_map/ppermute | solution.py:368
  50.9 1.4 %collective-permute-start.7 = (bf16[29,32,128]{2,1,0:T(8,128)(2,1)S(1)}, bf16[29,32,128]{2,1,0:T(8,128)(2,1)S(1)}, u32[]{:S(2)}, u32[]{:S(2)}) collective-permute-start(bf16[29,32,128]{2,1,0:T(8,128)(2,1)S(1)} %get-tuple-element.61), channel_id=1, source_target_pairs={{0,6},{1,7},{2,0},{3,1},{4,2},{5,3},{6,4},{7,5},{8,14},{9,15},{10,... | collective-permute-start | bytes 712712 | tf_op jit(solution)/shard_map/ppermute | solution.py:368
  52.4 3.7 %collective-permute-done.3.refs_3_ = bf16[29,32,128]{2,1,0:T(8,128)(2,1)S(1)} collective-permute-done((bf16[29,32,128]{2,1,0:T(8,128)(2,1)S(1)}, bf16[29,32,128]{2,1,0:T(8,128)(2,1)S(1)}, u32[]{:S(2)}, u32[]{:S(2)}) %collective-permute-start.3) | collective-permute-done | bytes 237600 | tf_op jit(solution)/shard_map/ppermute | solution.py:368
  56.0 1.2 collective-permute-start.8
  57.2 2.2 %collective-permute-start.9 = (bf16[29,32,128]{2,1,0:T(8,128)(2,1)S(1)}, bf16[29,32,128]{2,1,0:T(8,128)(2,1)S(1)}, u32[]{:S(2)}, u32[]{:S(2)}) collective-permute-start(bf16[29,32,128]{2,1,0:T(8,128)(2,1)S(1)} %get-tuple-element.63), channel_id=1, source_target_pairs={{0,4},{1,5},{2,6},{3,7},{4,0},{5,1},{6,2},{7,3},{8,12},{9,13},{10,... | collective-permute-start | bytes 712712 | tf_op jit(solution)/shard_map/ppermute | solution.py:368
  59.4 2.4 %collective-permute-start.10 = (bf16[29,32,128]{2,1,0:T(8,128)(2,1)}, bf16[29,32,128]{2,1,0:T(8,128)(2,1)}, u32[]{:S(2)}, u32[]{:S(2)}) collective-permute-start(bf16[29,32,128]{2,1,0:T(8,128)(2,1)} %get-tuple-element.64), channel_id=1, source_target_pairs={{0,15},{1,14},{2,9},{3,8},{4,11},{5,10},{6,13},{7,12},{8,7},{9,6},... | collective-permute-start | bytes 712712 | tf_op jit(solution)/shard_map/ppermute | solution.py:368
  62.1 1.6 %collective-permute-start.12 = (bf16[29,32,128]{2,1,0:T(8,128)(2,1)}, bf16[29,32,128]{2,1,0:T(8,128)(2,1)}, u32[]{:S(2)}, u32[]{:S(2)}) collective-permute-start(bf16[29,32,128]{2,1,0:T(8,128)(2,1)} %get-tuple-element.66), channel_id=1, source_target_pairs={{0,9},{1,8},{2,11},{3,10},{4,13},{5,12},{6,15},{7,14},{8,1},{9,0},... | collective-permute-start | bytes 712712 | tf_op jit(solution)/shard_map/ppermute | solution.py:368
  63.7 12.1 %collective-permute-done.8.refs_8_ = bf16[29,32,128]{2,1,0:T(8,128)(2,1)S(1)} collective-permute-done((bf16[29,32,128]{2,1,0:T(8,128)(2,1)S(1)}, bf16[29,32,128]{2,1,0:T(8,128)(2,1)S(1)}, u32[]{:S(2)}, u32[]{:S(2)}) %collective-permute-start.8) | collective-permute-done | bytes 237600 | tf_op jit(solution)/shard_map/ppermute | solution.py:368
  76.1 4.7 %collective-permute-done.9.refs_9_ = bf16[29,32,128]{2,1,0:T(8,128)(2,1)S(1)} collective-permute-done((bf16[29,32,128]{2,1,0:T(8,128)(2,1)S(1)}, bf16[29,32,128]{2,1,0:T(8,128)(2,1)S(1)}, u32[]{:S(2)}, u32[]{:S(2)}) %collective-permute-start.9) | collective-permute-done | bytes 237600 | tf_op jit(solution)/shard_map/ppermute | solution.py:368
  81.4 6.6 %rest.1 = (bf16[13,32,128]{2,1,0:T(8,128)(2,1)S(1)}, bf16[13,32,128]{2,1,0:T(8,128)(2,1)S(1)}, bf16[13,32,128]{2,1,0:T(8,128)(2,1)S(1)}, bf16[13,32,128]{2,1,0:T...) custom-call(s32[1]{0:T(128)} %bitcast.me_ref, ...), custom_call_target="tpu_custom_call" | custom-call | flops 1000000000 | bytes 10000000 | tf_op jit(solution)/shard_map/rest/pallas_call | solution.py:417
  89.9 1.7 %collective-permute-start.17 = (bf16[13,32,128]{2,1,0:T(8,128)(2,1)S(1)}, bf16[13,32,128]{2,1,0:T(8,128)(2,1)S(1)}, u32[]{:S(2)}, u32[]{:S(2)}) collective-permute-start(bf16[13,32,128]{2,1,0:T(8,128)(2,1)S(1)} %get-tuple-element.78), channel_id=1, source_target_pairs={{0,13},{1,12},{2,15},{3,14},{4,9},{5,8},{6,11},{7,10},{8,5},{9,4},... | collective-permute-start | bytes 319496 | tf_op jit(solution)/shard_map/ppermute | solution.py:368
  91.6 2.0 %collective-permute-start.18 = (bf16[13,32,128]{2,1,0:T(8,128)(2,1)S(1)}, bf16[13,32,128]{2,1,0:T(8,128)(2,1)S(1)}, u32[]{:S(2)}, u32[]{:S(2)}) collective-permute-start(bf16[13,32,128]{2,1,0:T(8,128)(2,1)S(1)} %get-tuple-element.79), channel_id=1, source_target_pairs={{0,12},{1,13},{2,14},{3,15},{4,8},{5,9},{6,10},{7,11},{8,4},{9,5},... | collective-permute-start | bytes 319496 | tf_op jit(solution)/shard_map/ppermute | solution.py:368
  93.7 2.0 %collective-permute-start.20 = (bf16[13,32,128]{2,1,0:T(8,128)(2,1)S(1)}, bf16[13,32,128]{2,1,0:T(8,128)(2,1)S(1)}, u32[]{:S(2)}, u32[]{:S(2)}) collective-permute-start(bf16[13,32,128]{2,1,0:T(8,128)(2,1)S(1)} %get-tuple-element.81), channel_id=1, source_target_pairs={{0,2},{1,3},{2,4},{3,5},{4,6},{5,7},{6,0},{7,1},{8,10},{9,11},{10,... | collective-permute-start | bytes 319496 | tf_op jit(solution)/shard_map/ppermute | solution.py:368
  97.4 1.3 collective-permute-start.22
  99.2 2.6 %collective-permute-start.24 = (bf16[13,32,128]{2,1,0:T(8,128)(2,1)}, bf16[13,32,128]{2,1,0:T(8,128)(2,1)S(1)}, u32[]{:S(2)}, u32[]{:S(2)}) collective-permute-start(bf16[13,32,128]{2,1,0:T(8,128)(2,1)} %get-tuple-element.85), channel_id=1, source_target_pairs={{0,6},{1,7},{2,0},{3,1},{4,2},{5,3},{6,4},{7,5},{8,14},{9,15},{10,... | collective-permute-start | bytes 319496 | tf_op jit(solution)/shard_map/ppermute | solution.py:368
  101.8 4.4 %collective-permute-done.20.refs_3_ = bf16[13,32,128]{2,1,0:T(8,128)(2,1)S(1)} collective-permute-done((bf16[13,32,128]{2,1,0:T(8,128)(2,1)S(1)}, bf16[13,32,128]{2,1,0:T(8,128)(2,1)S(1)}, u32[]{:S(2)}, u32[]{:S(2)}) %collective-permute-start.20) | collective-permute-done | bytes 106528 | tf_op jit(solution)/shard_map/ppermute | solution.py:368
  106.1 1.3 collective-permute-start.25
  107.4 1.9 %collective-permute-start.26 = (bf16[13,32,128]{2,1,0:T(8,128)(2,1)}, bf16[13,32,128]{2,1,0:T(8,128)(2,1)S(1)}, u32[]{:S(2)}, u32[]{:S(2)}) collective-permute-start(bf16[13,32,128]{2,1,0:T(8,128)(2,1)} %get-tuple-element.87), channel_id=1, source_target_pairs={{0,4},{1,5},{2,6},{3,7},{4,0},{5,1},{6,2},{7,3},{8,12},{9,13},{10,... | collective-permute-start | bytes 319496 | tf_op jit(solution)/shard_map/ppermute | solution.py:368
  111.5 2.4 %collective-permute-start.28 = (bf16[13,32,128]{2,1,0:T(8,128)(2,1)}, bf16[13,32,128]{2,1,0:T(8,128)(2,1)S(1)}, u32[]{:S(2)}, u32[]{:S(2)}) collective-permute-start(bf16[13,32,128]{2,1,0:T(8,128)(2,1)} %copy-done.4), channel_id=1, source_target_pairs={{0,14},{1,15},{2,8},{3,9},{4,10},{5,11},{6,12},{7,13},{8,6},{9,7},... | collective-permute-start | bytes 319496 | tf_op jit(solution)/shard_map/ppermute | solution.py:368
  113.9 1.2 collective-permute-start.29
  115.6 4.3 %collective-permute-done.26.refs_9_ = bf16[13,32,128]{2,1,0:T(8,128)(2,1)S(1)} collective-permute-done((bf16[13,32,128]{2,1,0:T(8,128)(2,1)}, bf16[13,32,128]{2,1,0:T(8,128)(2,1)S(1)}, u32[]{:S(2)}, u32[]{:S(2)}) %collective-permute-start.26) | collective-permute-done | bytes 106528 | tf_op jit(solution)/shard_map/ppermute | solution.py:368
  122.9 13.7 %join_first.1 = (bf16[48,32,2112]{2,1,0:T(8,128)(2,1)}, f32[48,1,2112]{2,1,0:T(1,128)}, s32[49]{0:T(128)S(1)}, s32[16]{0:T(128)S(1)}) custom-call(s32[1]{0:T(128)} %bitcast.me_ref, s32[16,28]{1,0:T(8,128)S(1)} %bitcast.11, s32[16]{0:T(128)S(1)} %get-tuple-element.53.inner_ref, bf16[29,32,128]{2,1,0:T(8,128)(2,1)S(1)} %collective-permute-done.refs_0_, ...), custom_call_target="tpu_custom_call" | custom-call | flops 4000000000 | bytes 10000000 | tf_op jit(solution)/shard_map/join_first/pallas_call | solution.py:448
  136.8 5.1 %join_last.1 = (bf16[48,32,2112]{2,1,0:T(8,128)(2,1)}, f32[48,1,2112]{2,1,0:T(1,128)}) custom-call(s32[1]{0:T(128)} %bitcast.me_ref, s32[49]{0:T(128)S(1)} %get-tuple-element.70.slot_ref, s32[16]{0:T(128)S(1)} %get-tuple-element.71.used_ref, s32[16]{0:T(128)S(1)} %get-tuple-element.72.end_ref, ...), custom_call_target="tpu_custom_call", output_to_operand_aliasing={{0}: (21, {}), {1}: (22, {})} | custom-call | flops 1000000000 | bytes 10000000 | tf_op jit(solution)/shard_map/join_last/pallas_call | solution.py:468
  (60 shorter events, 13.9 us)
Async XLA Ops:
  12.0 13.5 %collective-permute-start.15 = (bf16[17,32,128]{2,1,0:T(8,128)(2,1)S(1)}, bf16[17,32,128]{2,1,0:T(8,128)(2,1)S(1)}, u32[]{:S(2)}, u32[]{:S(2)}) collective-permute-start(bf16[17,32,128]{2,1,0:T(8,128)(2,1)S(1)} %get-tuple-element.76), channel_id=1, source_target_pairs={{0,16},{16,32},{32,48},{48,64},{64,80},{80,96},{96,112},{1,17},{17... | collective-permute-start | bytes 417800 | tf_op jit(solution)/shard_map/ppermute | solution.py:415
  15.8 10.8 %collective-permute-start.16 = (bf16[17,32,128]{2,1,0:T(8,128)(2,1)S(1)}, bf16[17,32,128]{2,1,0:T(8,128)(2,1)S(1)}, u32[]{:S(2)}, u32[]{:S(2)}) collective-permute-start(bf16[17,32,128]{2,1,0:T(8,128)(2,1)S(1)} %get-tuple-element.77), channel_id=1, source_target_pairs={{16,0},{32,16},{48,32},{64,48},{80,64},{96,80},{112,96},{17,1},{33... | collective-permute-start | bytes 417800 | tf_op jit(solution)/shard_map/ppermute | solution.py:416
  19.7 11.2 %collective-permute-start = (bf16[29,32,128]{2,1,0:T(8,128)(2,1)S(1)}, bf16[29,32,128]{2,1,0:T(8,128)(2,1)S(1)}, u32[]{:S(2)}, u32[]{:S(2)}) collective-permute-start(bf16[29,32,128]{2,1,0:T(8,128)(2,1)S(1)} %get-tuple-element.54), channel_id=1, source_target_pairs={{0,13},{1,12},{2,15},{3,14},{4,9},{5,8},{6,11},{7,10},{8,5},{9,4},... | collective-permute-start | bytes 712712 | tf_op jit(solution)/shard_map/ppermute | solution.py:368
  22.9 13.1 %collective-permute-start.1 = (bf16[29,32,128]{2,1,0:T(8,128)(2,1)S(1)}, bf16[29,32,128]{2,1,0:T(8,128)(2,1)S(1)}, u32[]{:S(2)}, u32[]{:S(2)}) collective-permute-start(bf16[29,32,128]{2,1,0:T(8,128)(2,1)S(1)} %get-tuple-element.55), channel_id=1, source_target_pairs={{0,12},{1,13},{2,14},{3,15},{4,8},{5,9},{6,10},{7,11},{8,4},{9,5},... | collective-permute-start | bytes 712712 | tf_op jit(solution)/shard_map/ppermute | solution.py:368
  24.8 26.2 %collective-permute-start.2 = (bf16[29,32,128]{2,1,0:T(8,128)(2,1)S(1)}, bf16[29,32,128]{2,1,0:T(8,128)(2,1)S(1)}, u32[]{:S(2)}, u32[]{:S(2)}) collective-permute-start(bf16[29,32,128]{2,1,0:T(8,128)(2,1)S(1)} %get-tuple-element.56), channel_id=1, source_target_pairs={{0,3},{1,2},{2,5},{3,4},{4,7},{5,6},{6,1},{7,0},{8,11},{9,10},{10,... | collective-permute-start | bytes 712712 | tf_op jit(solution)/shard_map/ppermute | solution.py:368
  25.5 30.5 %collective-permute-start.3 = (bf16[29,32,128]{2,1,0:T(8,128)(2,1)S(1)}, bf16[29,32,128]{2,1,0:T(8,128)(2,1)S(1)}, u32[]{:S(2)}, u32[]{:S(2)}) collective-permute-start(bf16[29,32,128]{2,1,0:T(8,128)(2,1)S(1)} %get-tuple-element.57), channel_id=1, source_target_pairs={{0,2},{1,3},{2,4},{3,5},{4,6},{5,7},{6,0},{7,1},{8,10},{9,11},{10,... | collective-permute-start | bytes 712712 | tf_op jit(solution)/shard_map/ppermute | solution.py:368
  26.5 30.7 %collective-permute-start.4 = (bf16[29,32,128]{2,1,0:T(8,128)(2,1)S(1)}, bf16[29,32,128]{2,1,0:T(8,128)(2,1)S(1)}, u32[]{:S(2)}, u32[]{:S(2)}) collective-permute-start(bf16[29,32,128]{2,1,0:T(8,128)(2,1)S(1)} %get-tuple-element.58), channel_id=1, source_target_pairs={{0,11},{1,10},{2,13},{3,12},{4,15},{5,14},{6,9},{7,8},{8,3},{9,2},... | collective-permute-start | bytes 712712 | tf_op jit(solution)/shard_map/ppermute | solution.py:368
  30.9 28.5 %collective-permute-start.5 = (bf16[29,32,128]{2,1,0:T(8,128)(2,1)S(1)}, bf16[29,32,128]{2,1,0:T(8,128)(2,1)S(1)}, u32[]{:S(2)}, u32[]{:S(2)}) collective-permute-start(bf16[29,32,128]{2,1,0:T(8,128)(2,1)S(1)} %get-tuple-element.59), channel_id=1, source_target_pairs={{0,10},{1,11},{2,12},{3,13},{4,14},{5,15},{6,8},{7,9},{8,2},{9,3},... | collective-permute-start | bytes 712712 | tf_op jit(solution)/shard_map/ppermute | solution.py:368
  36.0 25.8 %collective-permute-start.6 = (bf16[29,32,128]{2,1,0:T(8,128)(2,1)S(1)}, bf16[29,32,128]{2,1,0:T(8,128)(2,1)S(1)}, u32[]{:S(2)}, u32[]{:S(2)}) collective-permute-start(bf16[29,32,128]{2,1,0:T(8,128)(2,1)S(1)} %get-tuple-element.60), channel_id=1, source_target_pairs={{0,7},{1,6},{2,1},{3,0},{4,3},{5,2},{6,5},{7,4},{8,15},{9,14},{10,... | collective-permute-start | bytes 712712 | tf_op jit(solution)/shard_map/ppermute | solution.py:368
  50.9 11.2 %collective-permute-start.7 = (bf16[29,32,128]{2,1,0:T(8,128)(2,1)S(1)}, bf16[29,32,128]{2,1,0:T(8,128)(2,1)S(1)}, u32[]{:S(2)}, u32[]{:S(2)}) collective-permute-start(bf16[29,32,128]{2,1,0:T(8,128)(2,1)S(1)} %get-tuple-element.61), channel_id=1, source_target_pairs={{0,6},{1,7},{2,0},{3,1},{4,2},{5,3},{6,4},{7,5},{8,14},{9,15},{10,... | collective-permute-start | bytes 712712 | tf_op jit(solution)/shard_map/ppermute | solution.py:368
  56.0 19.8 %collective-permute-start.8 = (bf16[29,32,128]{2,1,0:T(8,128)(2,1)S(1)}, bf16[29,32,128]{2,1,0:T(8,128)(2,1)S(1)}, u32[]{:S(2)}, u32[]{:S(2)}) collective-permute-start(bf16[29,32,128]{2,1,0:T(8,128)(2,1)S(1)} %get-tuple-element.62), channel_id=1, source_target_pairs={{0,5},{1,4},{2,7},{3,6},{4,1},{5,0},{6,3},{7,2},{8,13},{9,12},{10,... | collective-permute-start | bytes 712712 | tf_op jit(solution)/shard_map/ppermute | solution.py:368
  57.2 23.6 %collective-permute-start.9 = (bf16[29,32,128]{2,1,0:T(8,128)(2,1)S(1)}, bf16[29,32,128]{2,1,0:T(8,128)(2,1)S(1)}, u32[]{:S(2)}, u32[]{:S(2)}) collective-permute-start(bf16[29,32,128]{2,1,0:T(8,128)(2,1)S(1)} %get-tuple-element.63), channel_id=1, source_target_pairs={{0,4},{1,5},{2,6},{3,7},{4,0},{5,1},{6,2},{7,3},{8,12},{9,13},{10,... | collective-permute-start | bytes 712712 | tf_op jit(solution)/shard_map/ppermute | solution.py:368
  59.4 30.5 %collective-permute-start.10 = (bf16[29,32,128]{2,1,0:T(8,128)(2,1)}, bf16[29,32,128]{2,1,0:T(8,128)(2,1)}, u32[]{:S(2)}, u32[]{:S(2)}) collective-permute-start(bf16[29,32,128]{2,1,0:T(8,128)(2,1)} %get-tuple-element.64), channel_id=1, source_target_pairs={{0,15},{1,14},{2,9},{3,8},{4,11},{5,10},{6,13},{7,12},{8,7},{9,6},... | collective-permute-start | bytes 712712 | tf_op jit(solution)/shard_map/ppermute | solution.py:368
  61.8 29.9 %collective-permute-start.11 = (bf16[29,32,128]{2,1,0:T(8,128)(2,1)}, bf16[29,32,128]{2,1,0:T(8,128)(2,1)}, u32[]{:S(2)}, u32[]{:S(2)}) collective-permute-start(bf16[29,32,128]{2,1,0:T(8,128)(2,1)} %get-tuple-element.65), channel_id=1, source_target_pairs={{0,14},{1,15},{2,8},{3,9},{4,10},{5,11},{6,12},{7,13},{8,6},{9,7},... | collective-permute-start | bytes 712712 | tf_op jit(solution)/shard_map/ppermute | solution.py:368
  62.1 31.5 %collective-permute-start.12 = (bf16[29,32,128]{2,1,0:T(8,128)(2,1)}, bf16[29,32,128]{2,1,0:T(8,128)(2,1)}, u32[]{:S(2)}, u32[]{:S(2)}) collective-permute-start(bf16[29,32,128]{2,1,0:T(8,128)(2,1)} %get-tuple-element.66), channel_id=1, source_target_pairs={{0,9},{1,8},{2,11},{3,10},{4,13},{5,12},{6,15},{7,14},{8,1},{9,0},... | collective-permute-start | bytes 712712 | tf_op jit(solution)/shard_map/ppermute | solution.py:368
  75.8 17.9 %collective-permute-start.13 = (bf16[29,32,128]{2,1,0:T(8,128)(2,1)}, bf16[29,32,128]{2,1,0:T(8,128)(2,1)}, u32[]{:S(2)}, u32[]{:S(2)}) collective-permute-start(bf16[29,32,128]{2,1,0:T(8,128)(2,1)} %get-tuple-element.67), channel_id=1, source_target_pairs={{0,8},{1,9},{2,10},{3,11},{4,12},{5,13},{6,14},{7,15},{8,0},{9,1},... | collective-permute-start | bytes 712712 | tf_op jit(solution)/shard_map/ppermute | solution.py:368
  80.8 14.9 %collective-permute-start.14 = (bf16[29,32,128]{2,1,0:T(8,128)(2,1)}, bf16[29,32,128]{2,1,0:T(8,128)(2,1)}, u32[]{:S(2)}, u32[]{:S(2)}) collective-permute-start(bf16[29,32,128]{2,1,0:T(8,128)(2,1)} %get-tuple-element.68), channel_id=1, source_target_pairs={{0,1},{1,0},{2,3},{3,2},{4,5},{5,4},{6,7},{7,6},{8,9},{9,8},{10,11... | collective-permute-start | bytes 712712 | tf_op jit(solution)/shard_map/ppermute | solution.py:368
  89.9 7.5 %collective-permute-start.17 = (bf16[13,32,128]{2,1,0:T(8,128)(2,1)S(1)}, bf16[13,32,128]{2,1,0:T(8,128)(2,1)S(1)}, u32[]{:S(2)}, u32[]{:S(2)}) collective-permute-start(bf16[13,32,128]{2,1,0:T(8,128)(2,1)S(1)} %get-tuple-element.78), channel_id=1, source_target_pairs={{0,13},{1,12},{2,15},{3,14},{4,9},{5,8},{6,11},{7,10},{8,5},{9,4},... | collective-permute-start | bytes 319496 | tf_op jit(solution)/shard_map/ppermute | solution.py:368
  91.6 7.4 %collective-permute-start.18 = (bf16[13,32,128]{2,1,0:T(8,128)(2,1)S(1)}, bf16[13,32,128]{2,1,0:T(8,128)(2,1)S(1)}, u32[]{:S(2)}, u32[]{:S(2)}) collective-permute-start(bf16[13,32,128]{2,1,0:T(8,128)(2,1)S(1)} %get-tuple-element.79), channel_id=1, source_target_pairs={{0,12},{1,13},{2,14},{3,15},{4,8},{5,9},{6,10},{7,11},{8,4},{9,5},... | collective-permute-start | bytes 319496 | tf_op jit(solution)/shard_map/ppermute | solution.py:368
  93.7 5.5 %collective-permute-start.19 = (bf16[13,32,128]{2,1,0:T(8,128)(2,1)S(1)}, bf16[13,32,128]{2,1,0:T(8,128)(2,1)S(1)}, u32[]{:S(2)}, u32[]{:S(2)}) collective-permute-start(bf16[13,32,128]{2,1,0:T(8,128)(2,1)S(1)} %get-tuple-element.80), channel_id=1, source_target_pairs={{0,3},{1,2},{2,5},{3,4},{4,7},{5,6},{6,1},{7,0},{8,11},{9,10},{10,... | collective-permute-start | bytes 319496 | tf_op jit(solution)/shard_map/ppermute | solution.py:368
  93.7 12.4 %collective-permute-start.20 = (bf16[13,32,128]{2,1,0:T(8,128)(2,1)S(1)}, bf16[13,32,128]{2,1,0:T(8,128)(2,1)S(1)}, u32[]{:S(2)}, u32[]{:S(2)}) collective-permute-start(bf16[13,32,128]{2,1,0:T(8,128)(2,1)S(1)} %get-tuple-element.81), channel_id=1, source_target_pairs={{0,2},{1,3},{2,4},{3,5},{4,6},{5,7},{6,0},{7,1},{8,10},{9,11},{10,... | collective-permute-start | bytes 319496 | tf_op jit(solution)/shard_map/ppermute | solution.py:368
  95.7 11.7 %collective-permute-start.21 = (bf16[13,32,128]{2,1,0:T(8,128)(2,1)S(1)}, bf16[13,32,128]{2,1,0:T(8,128)(2,1)S(1)}, u32[]{:S(2)}, u32[]{:S(2)}) collective-permute-start(bf16[13,32,128]{2,1,0:T(8,128)(2,1)S(1)} %get-tuple-element.82), channel_id=1, source_target_pairs={{0,11},{1,10},{2,13},{3,12},{4,15},{5,14},{6,9},{7,8},{8,3},{9,2},... | collective-permute-start | bytes 319496 | tf_op jit(solution)/shard_map/ppermute | solution.py:368
  97.4 13.2 %collective-permute-start.22 = (bf16[13,32,128]{2,1,0:T(8,128)(2,1)}, bf16[13,32,128]{2,1,0:T(8,128)(2,1)S(1)}, u32[]{:S(2)}, u32[]{:S(2)}) collective-permute-start(bf16[13,32,128]{2,1,0:T(8,128)(2,1)} %get-tuple-element.83), channel_id=1, source_target_pairs={{0,10},{1,11},{2,12},{3,13},{4,14},{5,15},{6,8},{7,9},{8,2},{9,3},... | collective-permute-start | bytes 319496 | tf_op jit(solution)/shard_map/ppermute | solution.py:368
  99.0 12.5 %collective-permute-start.23 = (bf16[13,32,128]{2,1,0:T(8,128)(2,1)}, bf16[13,32,128]{2,1,0:T(8,128)(2,1)S(1)}, u32[]{:S(2)}, u32[]{:S(2)}) collective-permute-start(bf16[13,32,128]{2,1,0:T(8,128)(2,1)} %get-tuple-element.84), channel_id=1, source_target_pairs={{0,7},{1,6},{2,1},{3,0},{4,3},{5,2},{6,5},{7,4},{8,15},{9,14},{10,... | collective-permute-start | bytes 319496 | tf_op jit(solution)/shard_map/ppermute | solution.py:368
  99.2 14.7 %collective-permute-start.24 = (bf16[13,32,128]{2,1,0:T(8,128)(2,1)}, bf16[13,32,128]{2,1,0:T(8,128)(2,1)S(1)}, u32[]{:S(2)}, u32[]{:S(2)}) collective-permute-start(bf16[13,32,128]{2,1,0:T(8,128)(2,1)} %get-tuple-element.85), channel_id=1, source_target_pairs={{0,6},{1,7},{2,0},{3,1},{4,2},{5,3},{6,4},{7,5},{8,14},{9,15},{10,... | collective-permute-start | bytes 319496 | tf_op jit(solution)/shard_map/ppermute | solution.py:368
  106.1 9.0 %collective-permute-start.25 = (bf16[13,32,128]{2,1,0:T(8,128)(2,1)}, bf16[13,32,128]{2,1,0:T(8,128)(2,1)S(1)}, u32[]{:S(2)}, u32[]{:S(2)}) collective-permute-start(bf16[13,32,128]{2,1,0:T(8,128)(2,1)} %get-tuple-element.86), channel_id=1, source_target_pairs={{0,5},{1,4},{2,7},{3,6},{4,1},{5,0},{6,3},{7,2},{8,13},{9,12},{10,... | collective-permute-start | bytes 319496 | tf_op jit(solution)/shard_map/ppermute | solution.py:368
  107.4 12.5 %collective-permute-start.26 = (bf16[13,32,128]{2,1,0:T(8,128)(2,1)}, bf16[13,32,128]{2,1,0:T(8,128)(2,1)S(1)}, u32[]{:S(2)}, u32[]{:S(2)}) collective-permute-start(bf16[13,32,128]{2,1,0:T(8,128)(2,1)} %get-tuple-element.87), channel_id=1, source_target_pairs={{0,4},{1,5},{2,6},{3,7},{4,0},{5,1},{6,2},{7,3},{8,12},{9,13},{10,... | collective-permute-start | bytes 319496 | tf_op jit(solution)/shard_map/ppermute | solution.py:368
  110.6 26.1 %collective-permute-start.27 = (bf16[13,32,128]{2,1,0:T(8,128)(2,1)}, bf16[13,32,128]{2,1,0:T(8,128)(2,1)S(1)}, u32[]{:S(2)}, u32[]{:S(2)}) collective-permute-start(bf16[13,32,128]{2,1,0:T(8,128)(2,1)} %copy-done.5), channel_id=1, source_target_pairs={{0,15},{1,14},{2,9},{3,8},{4,11},{5,10},{6,13},{7,12},{8,7},{9,6},... | collective-permute-start | bytes 319496 | tf_op jit(solution)/shard_map/ppermute | solution.py:368
  111.5 25.2 %collective-permute-start.28 = (bf16[13,32,128]{2,1,0:T(8,128)(2,1)}, bf16[13,32,128]{2,1,0:T(8,128)(2,1)S(1)}, u32[]{:S(2)}, u32[]{:S(2)}) collective-permute-start(bf16[13,32,128]{2,1,0:T(8,128)(2,1)} %copy-done.4), channel_id=1, source_target_pairs={{0,14},{1,15},{2,8},{3,9},{4,10},{5,11},{6,12},{7,13},{8,6},{9,7},... | collective-permute-start | bytes 319496 | tf_op jit(solution)/shard_map/ppermute | solution.py:368
  113.9 22.8 %collective-permute-start.29 = (bf16[13,32,128]{2,1,0:T(8,128)(2,1)}, bf16[13,32,128]{2,1,0:T(8,128)(2,1)S(1)}, u32[]{:S(2)}, u32[]{:S(2)}) collective-permute-start(bf16[13,32,128]{2,1,0:T(8,128)(2,1)} %copy-done.3), channel_id=1, source_target_pairs={{0,9},{1,8},{2,11},{3,10},{4,13},{5,12},{6,15},{7,14},{8,1},{9,0},... | collective-permute-start | bytes 319496 | tf_op jit(solution)/shard_map/ppermute | solution.py:368
  115.1 21.6 %collective-permute-start.30 = (bf16[13,32,128]{2,1,0:T(8,128)(2,1)S(1)}, bf16[13,32,128]{2,1,0:T(8,128)(2,1)S(1)}, u32[]{:S(2)}, u32[]{:S(2)}) collective-permute-start(bf16[13,32,128]{2,1,0:T(8,128)(2,1)S(1)} %get-tuple-element.91), channel_id=1, source_target_pairs={{0,8},{1,9},{2,10},{3,11},{4,12},{5,13},{6,14},{7,15},{8,0},{9,1},... | collective-permute-start | bytes 319496 | tf_op jit(solution)/shard_map/ppermute | solution.py:368
  119.9 16.8 %collective-permute-start.31 = (bf16[13,32,128]{2,1,0:T(8,128)(2,1)S(1)}, bf16[13,32,128]{2,1,0:T(8,128)(2,1)S(1)}, u32[]{:S(2)}, u32[]{:S(2)}) collective-permute-start(bf16[13,32,128]{2,1,0:T(8,128)(2,1)S(1)} %get-tuple-element.92), channel_id=1, source_target_pairs={{0,1},{1,0},{2,3},{3,2},{4,5},{5,4},{6,7},{7,6},{8,9},{9,8},{10,11... | collective-permute-start | bytes 319496 | tf_op jit(solution)/shard_map/ppermute | solution.py:368
  (11 other events, 127.9 us)
where the time goes:
time: 142 us
  starting transfers between devices  49.6 us (35%)
  waiting for transfers between devices  49.6 us (35%)
  Pallas kernels  35.4 us (25%)
  local copies, waits for them, and re-layouts  5.2 us (4%)
  between operations  1.63 us (1%)
    ppermute x30, waiting for transfers between devices, sent_to(): lax.ppermute(value, SERVE, [(i, ahead(i, offset)) for i in range(count)])  49.6 us
    ppermute x30, starting transfers between devices, sent_to(): lax.ppermute(value, SERVE, [(i, ahead(i, offset)) for i in range(count)])  41.9 us
    pallas_call x1, Pallas kernels, shards(): pl.pallas_call(join_first_kernel, in_specs=[in_smem()] * 3 + [anywhere()]...  13.7 us
    pallas_call x1, Pallas kernels, shards(): pl.pallas_call(turn_kernel, in_specs=[in_smem(), in_smem(), in_hbm()], ou...  9.97 us
    pallas_call x1, Pallas kernels, shards(): pl.pallas_call(rest_kernel, in_specs=[in_smem()] * 5 + [in_hbm()] + [in_v...  6.56 us
    unnamed x22, local copies, waits for them, and re-layouts  5.2 us
    pallas_call x1, Pallas kernels, shards(): pl.pallas_call(join_last_kernel, in_specs=[in_smem()] * 4 + [anywhere()]...  5.15 us
    ppermute x1, starting transfers between devices, shards(): lax.ppermute(head, 'train', [(i + 1, i) for i in range(train_n - 1)])  3.93 us
  transfers between devices with their start and end apart: 32, of which 11 were waited for; matrix products, arithmetic and copies ran while one was open for 0% of the time, Pallas kernels for 14%

commit v1 on v0

--- a/solution.py
+++ b/solution.py
@@ -1,3 +1,5 @@
+import functools
+
 import jax
 import jax.numpy as jnp
 from jax import lax
@@ -15,11 +17,13 @@
 SIDES = (2, 4, 2)
 OFFSETS = [
     (dx, dy, dc)
-    for dx, dy in ((1, 2), (0, 1), (1, 1), (0, 3), (0, 2), (1, 3), (1, 0), (0, 0))
-    for dc in (1, 0)
+    for dx, dy, dc in (
+        *((1, 2, 1), (1, 2, 0), (1, 1, 1), (0, 3, 1), (0, 1, 1), (1, 1, 0), (0, 1, 0), (0, 3, 0)),
+        *((1, 3, 1), (0, 2, 1), (0, 2, 0), (1, 3, 0), (1, 0, 1), (1, 0, 0), (0, 0, 1), (0, 0, 0)),
+    )
 ]
-LATER = sorted(range(len(OFFSETS)), key=lambda p: (-OFFSETS[p][0], p))
-FIRST, SECOND, THIRD = 28, 12, 20
+OPENING = 4
+FIRST, SECOND, THIRD = 31, 9, 23
 ENTRIES = 64
 NT = (((1,), (1,)), ((), ()))
 F32 = jnp.float32
@@ -78,10 +82,12 @@
     ref[size] = rest.astype(BF16)
 
 
-def turn_kernel(me_ref, group_ref, x_hbm, *refs):
-    peers = len(OFFSETS)
-    first_set, (rows_hbm, extra_ref, head_ref, tail_ref, table_ref, inner_ref, end_ref) = refs[:peers], refs[peers : peers + 7]
-    x_ref, planes, rows_ref, sems, out_sem = refs[peers + 7 :]
+def turn_kernel(me_ref, group_hbm, x_hbm, *refs):
+    set_hbm, refs = refs[:OPENING], refs[OPENING:]
+    rows_hbm, extra_ref, head_ref, tail_ref, table_ref, inner_ref, end_ref, most_ref = refs[:8]
+    x_ref, planes, rows_ref, first_set, group_ref, sems, out_sem, set_sem, group_sem = refs[8:]
+    load = pltpu.make_async_copy(group_hbm, group_ref, group_sem)
+    load.start()
     length = x_ref.shape[2]
     steps = LANES // PACK
     spare = PACK - 4
@@ -93,11 +99,11 @@
     ]
     for copy in copies:
         copy.start()
-    layers, blocks = group_ref.shape
+    layers, _, blocks = group_ref.shape
     groups = inner_ref.shape[0]
 
     def enter(count_ref, layer, b):
-        group = group_ref[layer, b]
+        group = group_ref[layer, 0, b]
         j = count_ref[group]
         count_ref[group] = j + 1
         table_ref[group * ENTRIES + j] = (layer << 10) + SHIFT + BLOCK * b
@@ -107,6 +113,7 @@
     perm = layer_major()
     me = me_ref[0]
     turns, part = me >> 2, 4 * (me & 3)
+    load.wait()
     copies[0].wait()
     for i in range(steps):
         copies[i + 1].wait()
@@ -126,6 +133,7 @@
     for layer in range(layers):
         for b in (0, blocks - 1):
             enter(end_ref, layer, b)
+    most_ref[0] = functools.reduce(jnp.maximum, [end_ref[g] for g in range(groups)])
 
     def layer_step(layer, carry):
         turned = jnp.transpose(planes[layer])
@@ -138,27 +146,48 @@
     lax.fori_loop(0, layers, layer_step, 0)
     head_ref[layers] = extra_ref[:SHIFT].astype(BF16)
     tail_ref[layers] = extra_ref[length - SHIFT :].astype(BF16)
-    for p, offset in enumerate(OFFSETS):
+    fill_first(OFFSETS[:OPENING], me, table_ref, inner_ref, extra_ref, rows_ref, first_set, set_hbm, set_sem)
+    pltpu.make_async_copy(rows_ref, rows_hbm, out_sem).wait()
+
+
+def fill_first(offsets, me, table_ref, inner_ref, extra_ref, rows_ref, first_set, set_hbm, set_sem):
+    stores = []
+    for p, offset in enumerate(offsets):
         group = ahead(me, offset)
         fill(
             (table_ref, extra_ref), me, group, 0, FIRST, inner_ref[group],
-            lambda layer, at: rows_ref[layer, pl.ds(at, BLOCK), :], first_set[p],
+            lambda layer, at: rows_ref[layer, pl.ds(at, BLOCK), :], first_set.at[p],
         )
-    pltpu.make_async_copy(rows_ref, rows_hbm, out_sem).wait()
-
-
-def rest_kernel(me_ref, shard_ref, offset_ref, table_ref, end_ref, rows_hbm, rest_ref, left_ref, right_ref, *refs):
-    peers = len(OFFSETS)
-    second_set, third_ref, (rows_ref, edge_ref, extra_ref, sem) = refs[:peers], refs[peers], refs[peers + 1 :]
+        stores.append(pltpu.make_async_copy(first_set.at[p], set_hbm[p], set_sem.at[p]))
+        stores[-1].start()
+    for store in stores:
+        store.wait()
+
+
+def first_kernel(me_ref, table_ref, inner_ref, rows_hbm, extra_ref, *refs):
+    offsets = OFFSETS[OPENING:]
+    set_hbm, (rows_ref, first_set, sem, set_sem) = refs[: len(offsets)], refs[len(offsets) :]
     load = pltpu.make_async_copy(rows_hbm, rows_ref, sem)
     load.start()
     load.wait()
-    layers, length = rows_ref.shape[:2]
+    fill_first(offsets, me_ref[0], table_ref, inner_ref, extra_ref, rows_ref, first_set, set_hbm, set_sem)
+
+
+def rest_kernel(me_ref, shard_ref, offset_ref, table_ref, end_ref, rows_hbm, rest_ref, left_ref, right_ref, *refs):
+    peers = len(OFFSETS)
+    second_hbm, third_hbm, rows_ref, edge_ref, extra_ref, second_ref, third_ref, sems, set_sem = refs
+    layers, length = rows_hbm.shape[:2]
     row = iota((BLOCK, LANES), 0)
     lane_group = iota((BLOCK, LANES), 1) >> 2
     me, shard = me_ref[0], shard_ref[0]
     last = length - 2 * SHIFT
     before = shard * (length - 2 * SHIFT)
+    cuts = (pl.ds(SHIFT, SHIFT), pl.ds(last, SHIFT), pl.ds(2 * SHIFT, last - 2 * SHIFT))
+    loads = [pltpu.make_async_copy(rows_hbm.at[:, cut], rows_ref.at[:, cut], sems.at[i]) for i, cut in enumerate(cuts)]
+    for load in loads:
+        load.start()
+    for load in loads[:2]:
+        load.wait()
 
     def edge_step(layer, carry):
         first, after = carry
@@ -179,14 +208,22 @@
         edge = edge_ref[layer, pl.ds(pl.multiple_of(jnp.where(high, SHIFT, 0), BLOCK), BLOCK), :]
         return jnp.where(low | high, edge, rows_ref[layer, pl.ds(at, BLOCK), :])
 
-    for p, offset in enumerate(OFFSETS):
-        group = ahead(me, offset)
-        fill((table_ref, extra_ref), me, group, FIRST, SECOND, end_ref[group], block, second_set[p])
+    loads[2].wait()
+    stores = []
+    for group in range(peers):
+        fill((table_ref, extra_ref), me, group, FIRST, SECOND, end_ref[group], block, second_ref.at[group])
+        stores.append(pltpu.make_async_copy(second_ref.at[group], second_hbm.at[group], set_sem.at[group]))
+        stores[-1].start()
+    for store in stores:
+        store.wait()
 
     def third_step(group, carry):
         @pl.when(end_ref[group] > FIRST + SECOND)
         def _():
-            fill((table_ref, extra_ref), me, group, FIRST + SECOND, THIRD, end_ref[group], block, third_ref.at[group])
+            fill((table_ref, extra_ref), me, group, FIRST + SECOND, THIRD, end_ref[group], block, third_ref)
+            store = pltpu.make_async_copy(third_ref, third_hbm.at[group], sems.at[3])
+            store.start()
+            store.wait()
 
         return carry
 
@@ -216,9 +253,7 @@
         code_ref[:, LANES * t : LANES * t + size] = (x * (1.0 / top)).astype(BF16)[:, :size]
 
 
-def write_slots(slot_ref, used_ref, codes_hbm, scale_hbm, code_ref, scale_ref, code_sem, scale_sem, low, high, compute):
-    layers = used_ref.shape[0]
-    per_layer = codes_hbm.shape[0] // layers
+def write_slots(codes_hbm, scale_hbm, code_ref, scale_ref, code_sem, scale_sem, low, high, slot_of, compute):
     ring = code_ref.shape[0]
 
     def stores(i, slot):
@@ -227,41 +262,38 @@
             pltpu.make_async_copy(scale_ref.at[i], scale_hbm.at[slot], scale_sem.at[i]),
         )
 
-    def layer_step(layer, done):
-        for k in range(per_layer):
-            j = slot_ref[per_layer * layer + k]
-            mine = (k < used_ref[layer]) & (j >= low) & (j < high)
-            i = done & (ring - 1)
-
-            @pl.when(mine)
-            def _(j=j, i=i, done=done, k=k):
-                @pl.when(done >= ring)
-                def _():
-                    for store in stores(i, 0):
-                        store.wait()
-
-                compute(j, code_ref.at[i], scale_ref.at[i])
-                for store in stores(i, per_layer * layer + k):
-                    store.start()
-
-            done = done + mine.astype(jnp.int32)
-        return done
-
-    done = lax.fori_loop(0, layers, layer_step, jnp.int32(0))
+    def step(j, carry):
+        i = j - low & (ring - 1)
+
+        @pl.when(j - low >= ring)
+        def _():
+            for store in stores(i, 0):
+                store.wait()
+
+        compute(j, code_ref.at[i], scale_ref.at[i])
+        for store in stores(i, slot_of(j)):
+            store.start()
+        return carry
+
+    lax.fori_loop(low, high, step, 0)
     for i in range(ring):
 
-        @pl.when(done > i)
+        @pl.when(high - low > i)
         def _(i=i):
             for store in stores(i, 0):
                 store.wait()
 
 
-def join_first_kernel(me_ref, group_ref, inner_ref, *refs):
+def join_first_kernel(me_ref, group_hbm, inner_ref, *refs):
     peers = len(OFFSETS)
-    parts, (codes_hbm, scale_hbm, slot_ref, used_ref) = refs[:peers], refs[peers : peers + 4]
-    held, code_ref, scale_ref, zero_code, zero_scale, sems, code_sem, scale_sem, zero_sem = refs[peers + 4 :]
+    parts, (codes_hbm, scale_hbm, late_ref) = refs[:peers], refs[peers : peers + 3]
+    held, code_ref, scale_ref, zero_code, zero_scale, group_ref, slot_ref, used_ref = refs[peers + 3 : peers + 11]
+    sems, code_sem, scale_sem, zero_sem = refs[peers + 11 :]
     me, width = me_ref[0], codes_hbm.shape[2]
-    layers, blocks = group_ref.shape
+    layers, _, blocks = group_ref.shape
+    load = pltpu.make_async_copy(group_hbm, group_ref, sems.at[peers])
+    load.start()
+    load.wait()
     per_layer = codes_hbm.shape[0] // layers
     loads = [pltpu.make_async_copy(part, held.at[behind(me, o)], sems.at[p]) for p, (part, o) in enumerate(zip(parts, OFFSETS))]
     for load in loads:
@@ -269,19 +301,25 @@
     zero_code[...] = jnp.zeros_like(zero_code)
     zero_scale[...] = jnp.zeros_like(zero_scale)
 
+    unused = ENTRIES
+
     def find(layer, carry):
         inner, edge = carry
         k = jnp.int32(0)
         for b in range(blocks):
-            mine = (group_ref[layer, b] == me).astype(jnp.int32)
+            mine = (group_ref[layer, 0, b] == me).astype(jnp.int32)
             at_edge = b in (0, blocks - 1)
-            slot_ref[jnp.where(mine == 1, per_layer * layer + k, per_layer * layers)] = edge if at_edge else inner
+            slot_ref[jnp.where(mine == 1, edge if at_edge else inner, unused)] = per_layer * layer + k
             k = k + mine
             inner, edge = (inner, edge + mine) if at_edge else (inner + mine, edge)
         used_ref[layer] = k
         return inner, edge
 
-    lax.fori_loop(0, layers, find, (jnp.int32(0), jnp.maximum(inner_ref[me], FIRST)))
+    inner, edge = lax.fori_loop(0, layers, find, (jnp.int32(0), jnp.maximum(inner_ref[me], FIRST)))
+    for j in range(FIRST, ENTRIES):
+        late_ref[j - FIRST] = slot_ref[j]
+    late_ref[ENTRIES - FIRST] = edge
+    late_ref[ENTRIES - FIRST + 1] = me
 
     def clear(slot):
         return (
@@ -309,37 +347,34 @@
     def compute(j, code, scale):
         join_slot(held, j, FIRST, j, code, scale, width)
 
-    write_slots(slot_ref, used_ref, codes_hbm, scale_hbm, code_ref, scale_ref, code_sem, scale_sem, 0, FIRST, compute)
+    write_slots(
+        codes_hbm, scale_hbm, code_ref, scale_ref, code_sem, scale_sem,
+        0, jnp.minimum(inner, FIRST), lambda j: slot_ref[j], compute,
+    )
     each_empty(lambda copy: copy.wait())
 
 
-def join_last_kernel(me_ref, slot_ref, used_ref, end_ref, *refs):
-    peers = len(OFFSETS)
-    parts, third_hbm, (codes_hbm, scale_hbm) = refs[:peers], refs[peers], refs[peers + 3 : peers + 5]
-    held, code_ref, scale_ref, sems, code_sem, scale_sem = refs[peers + 5 :]
-    me, width = me_ref[0], codes_hbm.shape[2]
-    loads = [
-        pltpu.make_async_copy(part, held.at[behind(me, o), pl.ds(0, SECOND + 1)], sems.at[p])
-        for p, (part, o) in enumerate(zip(parts, OFFSETS))
-    ]
-    for load in loads:
-        load.start()
-
-    @pl.when(end_ref[me] > FIRST + SECOND)
+def join_last_kernel(late_ref, second_hbm, third_hbm, *refs):
+    codes_hbm, scale_hbm, held, code_ref, scale_ref, sems, code_sem, scale_sem = refs[2:]
+    end, width = late_ref[ENTRIES - FIRST], codes_hbm.shape[2]
+    second = pltpu.make_async_copy(second_hbm, held.at[:, pl.ds(0, SECOND + 1)], sems.at[0])
+    second.start()
+
+    @pl.when(end > FIRST + SECOND)
     def _():
-        load = pltpu.make_async_copy(third_hbm, held.at[:, pl.ds(SECOND + 1, THIRD + 1)], sems.at[peers])
+        load = pltpu.make_async_copy(third_hbm, held.at[:, pl.ds(SECOND + 1, THIRD + 1)], sems.at[1])
         load.start()
         load.wait()
 
-    for load in loads:
-        load.wait()
+    second.wait()
 
     def compute(j, code, scale):
         late = (j >= FIRST + SECOND).astype(jnp.int32)
         join_slot(held, j - FIRST + late, SECOND + late * (THIRD + 1), j & 31, code, scale, width)
 
     write_slots(
-        slot_ref, used_ref, codes_hbm, scale_hbm, code_ref, scale_ref, code_sem, scale_sem, FIRST, ENTRIES, compute
+        codes_hbm, scale_hbm, code_ref, scale_ref, code_sem, scale_sem,
+        FIRST, end, lambda j: late_ref[j - FIRST], compute,
     )
 
 
@@ -378,7 +413,7 @@
     per_layer = (blocks_dev + serve_n - 1) // serve_n + 1
     slots = layers * per_layer
     width = columns * serve_n
-    groups = block_group[:, :, 0]
+    groups = hbm(jnp.transpose(block_group, (0, 2, 1)))
     me, shard = serve_idx.reshape(1), train_idx.astype(jnp.int32).reshape(1)
     by_column = hbm(jnp.transpose(train_weights, (2, 0, 1)))
 
@@ -388,9 +423,9 @@
     per_group = jax.ShapeDtypeStruct((serve_n,), jnp.int32)
     turned = pl.pallas_call(
         turn_kernel,
-        in_specs=[in_smem(), in_smem(), in_hbm()],
-        out_specs=[in_vmem()] * peers + [in_hbm()] + [in_vmem()] * 3 + [in_smem()] * 3,
-        out_shape=[jax.ShapeDtypeStruct((FIRST + 1, BLOCK, LANES), BF16)] * peers
+        in_specs=[in_smem(), in_hbm(), in_hbm()],
+        out_specs=[in_hbm()] * (OPENING + 1) + [in_vmem()] * 3 + [in_smem()] * 4,
+        out_shape=[pltpu.HBM((FIRST + 1, BLOCK, LANES), BF16)] * OPENING
         + [
             pltpu.HBM((layers, buffer_len, LANES), BF16),
             jax.ShapeDtypeStruct((buffer_len, LANES), F32),
@@ -399,64 +434,87 @@
             jax.ShapeDtypeStruct((serve_n * ENTRIES,), jnp.int32),
             per_group,
             per_group,
+            jax.ShapeDtypeStruct((1,), jnp.int32),
         ],
         scratch_shapes=[
             pltpu.VMEM((columns + PACK - 4, layers, buffer_len), BF16),
             pltpu.VMEM((layers, LANES, buffer_len), BF16),
             pltpu.VMEM((layers, buffer_len, LANES), BF16),
+            pltpu.VMEM((OPENING, FIRST + 1, BLOCK, LANES), BF16),
+            pltpu.SMEM((layers, 1, blocks_dev), jnp.int32),
             pltpu.SemaphoreType.DMA((steps + 2,)),
+            pltpu.SemaphoreType.DMA,
+            pltpu.SemaphoreType.DMA((OPENING,)),
             pltpu.SemaphoreType.DMA,
         ],
         compiler_params=pltpu.CompilerParams(vmem_limit_bytes=24 * MIB),
         cost_estimate=pl.CostEstimate(flops=3 * 10**9, bytes_accessed=9 * 10**6, transcendentals=0),
         name="turn",
     )(me, groups, by_column)
-    first_sent, (rows, rest, head, tail, table, inner, end) = turned[:peers], turned[peers:]
+    rows, rest, head, tail, table, inner, end, most = turned[OPENING:]
+    others = peers - OPENING
+    first_sent = turned[:OPENING] + pl.pallas_call(
+        first_kernel,
+        in_specs=[in_smem()] * 3 + [in_hbm(), in_vmem()],
+        out_specs=[in_hbm()] * others,
+        out_shape=[pltpu.HBM((FIRST + 1, BLOCK, LANES), BF16)] * others,
+        scratch_shapes=[
+            pltpu.VMEM((layers, buffer_len, LANES), BF16),
+            pltpu.VMEM((others, FIRST + 1, BLOCK, LANES), BF16),
+            pltpu.SemaphoreType.DMA,
+            pltpu.SemaphoreType.DMA((others,)),
+        ],
+        compiler_params=pltpu.CompilerParams(vmem_limit_bytes=16 * MIB),
+        cost_estimate=pl.CostEstimate(flops=10**9, bytes_accessed=10**7, transcendentals=0),
+        name="first_set",
+    )(me, table, inner, hbm(rows), rest)
     left = lax.ppermute(tail, "train", [(i, i + 1) for i in range(train_n - 1)])
     right = lax.ppermute(head, "train", [(i + 1, i) for i in range(train_n - 1)])
-    *second_sent, third_sent = pl.pallas_call(
+    second_sent, third_sent = pl.pallas_call(
         rest_kernel,
         in_specs=[in_smem()] * 5 + [in_hbm()] + [in_vmem()] * 3,
-        out_specs=[in_vmem()] * (peers + 1),
-        out_shape=[jax.ShapeDtypeStruct((SECOND + 1, BLOCK, LANES), BF16)] * peers
-        + [jax.ShapeDtypeStruct((serve_n, THIRD + 1, BLOCK, LANES), BF16)],
+        out_specs=[in_hbm(), in_hbm()],
+        out_shape=[pltpu.HBM((serve_n, n + 1, BLOCK, LANES), BF16) for n in (SECOND, THIRD)],
         scratch_shapes=[
             pltpu.VMEM((layers, buffer_len, LANES), BF16),
             pltpu.VMEM((layers, 2 * SHIFT, LANES), BF16),
             pltpu.VMEM((buffer_len, LANES), F32),
-            pltpu.SemaphoreType.DMA,
+            pltpu.VMEM((serve_n, SECOND + 1, BLOCK, LANES), BF16),
+            pltpu.VMEM((THIRD + 1, BLOCK, LANES), BF16),
+            pltpu.SemaphoreType.DMA((4,)),
+            pltpu.SemaphoreType.DMA((serve_n,)),
         ],
         compiler_params=pltpu.CompilerParams(vmem_limit_bytes=16 * MIB),
         cost_estimate=pl.CostEstimate(flops=10**9, bytes_accessed=10**7, transcendentals=0),
         name="rest",
     )(me, shard, row_offset, table, end, hbm(rows), rest, left, right)
 
-    got_first = [sent_to(v, o) for v, o in zip(first_sent[:-1], OFFSETS)] + [first_sent[-1]]
-    got_second = list(second_sent)
-    for p in LATER:
-        if p < peers - 1:
-            got_second[p] = sent_to(second_sent[p], OFFSETS[p])
+    got_first = [sent_to(v, o) for v, o in zip(first_sent[:OPENING], OFFSETS)]
+    got_first += [sent_to(v, o) for v, o in zip(first_sent[OPENING:-1], OFFSETS[OPENING:])] + [first_sent[-1]]
+    got_second = lax.all_to_all(second_sent, SERVE, split_axis=0, concat_axis=0, tiled=True)
     got_third = lax.cond(
-        jnp.max(end) > FIRST + SECOND,
+        most.reshape(()) > FIRST + SECOND,
         lambda v: lax.all_to_all(v, SERVE, split_axis=0, concat_axis=0, tiled=True),
         lambda v: v,
         third_sent,
     )
-    ring = 4
+    ring = 8
     results = [pltpu.HBM((slots, BLOCK, width), BF16), pltpu.HBM((slots, 1, width), F32)]
     buffers = [pltpu.VMEM((ring, BLOCK, width), BF16), pltpu.VMEM((ring, 1, width), F32)]
-    codes, scales, slot_of, used = pl.pallas_call(
+    codes, scales, late = pl.pallas_call(
         join_first_kernel,
-        in_specs=[in_smem()] * 3 + [anywhere()] * peers,
-        out_specs=[in_hbm(), in_hbm(), in_smem(), in_smem()],
-        out_shape=results
-        + [jax.ShapeDtypeStruct((slots + 1,), jnp.int32), jax.ShapeDtypeStruct((layers,), jnp.int32)],
+        in_specs=[in_smem(), in_hbm(), in_smem()] + [in_hbm()] * (peers - 1) + [anywhere()],
+        out_specs=[in_hbm(), in_hbm(), in_smem()],
+        out_shape=results + [jax.ShapeDtypeStruct((ENTRIES - FIRST + 2,), jnp.int32)],
         scratch_shapes=[
             pltpu.VMEM((serve_n, FIRST + 1, BLOCK, LANES), BF16),
             *buffers,
             pltpu.VMEM((BLOCK, width), BF16),
             pltpu.VMEM((1, width), F32),
-            pltpu.SemaphoreType.DMA((peers,)),
+            pltpu.SMEM((layers, 1, blocks_dev), jnp.int32),
+            pltpu.SMEM((ENTRIES + 1,), jnp.int32),
+            pltpu.SMEM((layers,), jnp.int32),
+            pltpu.SemaphoreType.DMA((peers + 1,)),
             pltpu.SemaphoreType.DMA((ring,)),
             pltpu.SemaphoreType.DMA((ring,)),
             pltpu.SemaphoreType.DMA((2,)),
@@ -464,24 +522,24 @@
         compiler_params=pltpu.CompilerParams(vmem_limit_bytes=16 * MIB),
         cost_estimate=pl.CostEstimate(flops=4 * 10**9, bytes_accessed=10**7, transcendentals=0),
         name="join_first",
-    )(me, groups, inner, *got_first)
+    )(me, groups, inner, *map(hbm, got_first[:-1]), got_first[-1])
     codes, scales = pl.pallas_call(
         join_last_kernel,
-        in_specs=[in_smem()] * 4 + [anywhere()] * (peers + 1) + [in_hbm()] * 2,
+        in_specs=[in_smem(), anywhere()] + [in_hbm()] * 3,
         out_specs=[in_hbm(), in_hbm()],
         out_shape=results,
-        input_output_aliases={peers + 5: 0, peers + 6: 1},
+        input_output_aliases={3: 0, 4: 1},
         scratch_shapes=[
             pltpu.VMEM((serve_n, SECOND + THIRD + 2, BLOCK, LANES), BF16),
             *buffers,
-            pltpu.SemaphoreType.DMA((peers + 1,)),
+            pltpu.SemaphoreType.DMA((2,)),
             pltpu.SemaphoreType.DMA((ring,)),
             pltpu.SemaphoreType.DMA((ring,)),
         ],
         compiler_params=pltpu.CompilerParams(vmem_limit_bytes=16 * MIB),
         cost_estimate=pl.CostEstimate(flops=10**9, bytes_accessed=10**7, transcendentals=0),
         name="join_last",
-    )(me, slot_of, used, end, *got_second, got_third, codes, scales)
+    )(late, got_second, hbm(got_third), codes, scales)
     return (
         codes.reshape(layers, 1, 1, per_layer, BLOCK, width),
         scales.reshape(layers, 1, 1, per_layer, width),

time: 142 us -> 107 us (0.75)
  the two profiles are of different devices: /device:TPU:43 before, /device:TPU:96 now
where the time goes in v1:
time: 107 us
  waiting for transfers between devices  40.6 us (38%)
  starting transfers between devices  32.4 us (30%)
  Pallas kernels  30.8 us (29%)
  local copies, waits for them, and re-layouts  1.69 us (2%)
  between operations  1.44 us (1%)
    ppermute x15, waiting for transfers between devices, sent_to(): lax.ppermute(value, SERVE, [(i, ahead(i, offset)) for i in range(count)])  40.6 us
    ppermute x15, starting transfers between devices, sent_to(): lax.ppermute(value, SERVE, [(i, ahead(i, offset)) for i in range(count)])  20.2 us
    pallas_call x1, Pallas kernels, shards(): pl.pallas_call(join_first_kernel, in_specs=[in_smem(), in_hbm(), in_smem(...  9.87 us
    pallas_call x1, Pallas kernels, shards(): pl.pallas_call(turn_kernel, in_specs=[in_smem(), in_hbm(), in_hbm()], out...  8.46 us
    pallas_call x1, Pallas kernels, shards(): pl.pallas_call(first_kernel, in_specs=[in_smem()] * 3 + [in_hbm(), in_vme...  5.57 us
    pallas_call x1, Pallas kernels, shards(): pl.pallas_call(rest_kernel, in_specs=[in_smem()] * 5 + [in_hbm()] + [in_v...  4.95 us
    ppermute x1, starting transfers between devices, shards(): left = lax.ppermute(tail, 'train', [(i, i + 1) for i in range(train_n - 1)])  4.94 us
    all_to_all x1, starting transfers between devices, shards(): lax.all_to_all(second_sent, SERVE, split_axis=0, concat_axis=0, tiled=True)  3.93 us
  transfers between devices with their start and end apart: 18, of which 6 were waited for; matrix products, arithmetic and copies ran while one was open for 0% of the time, Pallas kernels for 19%

profile of v1, /device:TPU:96, one launch (start us, length us, event | category | flops | bytes accessed | tf_op | source)
XLA Modules:
  0.0 106.9 jit_solution(6290244841151641954)
XLA Ops:
  0.6 8.5 %turn.1 = (bf16[32,32,128]{2,1,0:T(8,128)(2,1)}, bf16[32,32,128]{2,1,0:T(8,128)(2,1)}, bf16[32,32,128]{2,1,0:T(8,128)(2,1)}, bf16[32,32,128]{2,1,0:T(8,128)(2,1)...) custom-call(s32[1]{0:T(128)} %bitcast.me_ref, ...), custom_call_target="tpu_custom_call" | custom-call | flops 3000000000 | bytes 9000000 | tf_op jit(solution)/shard_map/turn/pallas_call | solution.py:424
  9.1 4.9 %collective-permute-start.15 = (bf16[17,32,128]{2,1,0:T(8,128)(2,1)S(1)}, bf16[17,32,128]{2,1,0:T(8,128)(2,1)S(1)}, u32[]{:S(2)}, u32[]{:S(2)}) collective-permute-start(bf16[17,32,128]{2,1,0:T(8,128)(2,1)S(1)} %get-tuple-element.60), channel_id=1, source_target_pairs={{0,16},{16,32},{32,48},{48,64},{64,80},{80,96},{96,112},{1,17},{17... | collective-permute-start | bytes 417800 | tf_op jit(solution)/shard_map/ppermute | solution.py:471
  14.1 3.3 %collective-permute-start.16 = (bf16[17,32,128]{2,1,0:T(8,128)(2,1)S(1)}, bf16[17,32,128]{2,1,0:T(8,128)(2,1)S(1)}, u32[]{:S(2)}, u32[]{:S(2)}) collective-permute-start(bf16[17,32,128]{2,1,0:T(8,128)(2,1)S(1)} %get-tuple-element.61), channel_id=1, source_target_pairs={{16,0},{32,16},{48,32},{64,48},{80,64},{96,80},{112,96},{17,1},{33... | collective-permute-start | bytes 417800 | tf_op jit(solution)/shard_map/ppermute | solution.py:472
  17.4 3.1 %collective-permute-start = (bf16[32,32,128]{2,1,0:T(8,128)(2,1)}, bf16[32,32,128]{2,1,0:T(8,128)(2,1)S(1)}, u32[]{:S(2)}, u32[]{:S(2)}) collective-permute-start(bf16[32,32,128]{2,1,0:T(8,128)(2,1)} %get-tuple-element.39), channel_id=1, source_target_pairs={{0,13},{1,12},{2,15},{3,14},{4,9},{5,8},{6,11},{7,10},{8,5},{9,4},... | collective-permute-start | bytes 786440 | tf_op jit(solution)/shard_map/ppermute | solution.py:403
  20.5 1.2 %collective-permute-start.1 = (bf16[32,32,128]{2,1,0:T(8,128)(2,1)}, bf16[32,32,128]{2,1,0:T(8,128)(2,1)S(1)}, u32[]{:S(2)}, u32[]{:S(2)}) collective-permute-start(bf16[32,32,128]{2,1,0:T(8,128)(2,1)} %get-tuple-element.40), channel_id=1, source_target_pairs={{0,12},{1,13},{2,14},{3,15},{4,8},{5,9},{6,10},{7,11},{8,4},{9,5},... | collective-permute-start | bytes 786440 | tf_op jit(solution)/shard_map/ppermute | solution.py:403
  21.7 2.2 %collective-permute-start.2 = (bf16[32,32,128]{2,1,0:T(8,128)(2,1)}, bf16[32,32,128]{2,1,0:T(8,128)(2,1)S(1)}, u32[]{:S(2)}, u32[]{:S(2)}) collective-permute-start(bf16[32,32,128]{2,1,0:T(8,128)(2,1)} %get-tuple-element.41), channel_id=1, source_target_pairs={{0,11},{1,10},{2,13},{3,12},{4,15},{5,14},{6,9},{7,8},{8,3},{9,2},... | collective-permute-start | bytes 786440 | tf_op jit(solution)/shard_map/ppermute | solution.py:403
  24.4 0.0 collective-permute-done.15.left_ref
  24.4 0.9 collective-permute-start.3
  25.3 5.0 %rest.1 = (bf16[16,10,32,128]{3,2,1,0:T(8,128)(2,1)}, bf16[16,24,32,128]{3,2,1,0:T(8,128)(2,1)}) custom-call(s32[1]{0:T(128)} %bitcast.me_ref, s32[1]{0:T(128)} %bitcast.3.shard_ref, s32[16,9]{1,0:T(8,128)S(1)} %copy-done, s32[1024]{0:T(1024)S(1)} %get-tuple-element.43.table_ref, s32[16]{0:T(128)S(1)} %get-tuple-element.59.end_ref, ...), custom_call_target="tpu_custom_call" | custom-call | flops 1000000000 | bytes 10000000 | tf_op jit(solution)/shard_map/rest/pallas_call | solution.py:473
  30.3 3.9 %all-to-all-start.1 = ((bf16[16,10,32,128]{3,2,1,0:T(8,128)(2,1)}), bf16[16,10,32,128]{3,2,1,0:T(8,128)(2,1)S(1)}, u32[]{:S(2)}, u32[]{:S(2)}) async-start(bf16[16,10,32,128]{3,2,1,0:T(8,128)(2,1)} %get-tuple-element.62), calls=%async_computation.1 | async-start | bytes 2621440 | tf_op jit(solution)/shard_map/all_to_all | solution.py:494
  34.2 5.6 %first_set.1 = (bf16[32,32,128]{2,1,0:T(8,128)(2,1)}, bf16[32,32,128]{2,1,0:T(8,128)(2,1)}, bf16[32,32,128]{2,1,0:T(8,128)(2,1)}, bf16[32,32,128]{2,1,0:T(8,128)...) custom-call(s32[1]{0:T(128)} %bitcast.me_ref, ...), custom_call_target="tpu_custom_call" | custom-call | flops 1000000000 | bytes 10000000 | tf_op jit(solution)/shard_map/first_set/pallas_call | solution.py:456
  39.8 1.7 %collective-permute-start.4 = (bf16[32,32,128]{2,1,0:T(8,128)(2,1)}, bf16[32,32,128]{2,1,0:T(8,128)(2,1)S(1)}, u32[]{:S(2)}, u32[]{:S(2)}) collective-permute-start(bf16[32,32,128]{2,1,0:T(8,128)(2,1)} %get-tuple-element.46), channel_id=1, source_target_pairs={{0,3},{1,2},{2,5},{3,4},{4,7},{5,6},{6,1},{7,0},{8,11},{9,10},{10,... | collective-permute-start | bytes 786440 | tf_op jit(solution)/shard_map/ppermute | solution.py:403
  41.5 2.4 %collective-permute-start.5 = (bf16[32,32,128]{2,1,0:T(8,128)(2,1)}, bf16[32,32,128]{2,1,0:T(8,128)(2,1)S(1)}, u32[]{:S(2)}, u32[]{:S(2)}) collective-permute-start(bf16[32,32,128]{2,1,0:T(8,128)(2,1)} %get-tuple-element.47), channel_id=1, source_target_pairs={{0,10},{1,11},{2,12},{3,13},{4,14},{5,15},{6,8},{7,9},{8,2},{9,3},... | collective-permute-start | bytes 786440 | tf_op jit(solution)/shard_map/ppermute | solution.py:403
  43.9 1.2 %collective-permute-start.6 = (bf16[32,32,128]{2,1,0:T(8,128)(2,1)}, bf16[32,32,128]{2,1,0:T(8,128)(2,1)S(1)}, u32[]{:S(2)}, u32[]{:S(2)}) collective-permute-start(bf16[32,32,128]{2,1,0:T(8,128)(2,1)} %get-tuple-element.48), channel_id=1, source_target_pairs={{0,2},{1,3},{2,4},{3,5},{4,6},{5,7},{6,0},{7,1},{8,10},{9,11},{10,... | collective-permute-start | bytes 786440 | tf_op jit(solution)/shard_map/ppermute | solution.py:403
  45.1 2.1 %collective-permute-start.7 = (bf16[32,32,128]{2,1,0:T(8,128)(2,1)}, bf16[32,32,128]{2,1,0:T(8,128)(2,1)S(1)}, u32[]{:S(2)}, u32[]{:S(2)}) collective-permute-start(bf16[32,32,128]{2,1,0:T(8,128)(2,1)} %get-tuple-element.49), channel_id=1, source_target_pairs={{0,6},{1,7},{2,0},{3,1},{4,2},{5,3},{6,4},{7,5},{8,14},{9,15},{10,... | collective-permute-start | bytes 786440 | tf_op jit(solution)/shard_map/ppermute | solution.py:403
  47.2 19.8 %collective-permute-done.4.refs_4_ = bf16[32,32,128]{2,1,0:T(8,128)(2,1)S(1)} collective-permute-done((bf16[32,32,128]{2,1,0:T(8,128)(2,1)}, bf16[32,32,128]{2,1,0:T(8,128)(2,1)S(1)}, u32[]{:S(2)}, u32[]{:S(2)}) %collective-permute-start.4) | collective-permute-done | bytes 262176 | tf_op jit(solution)/shard_map/ppermute | solution.py:403
  67.0 0.6 collective-permute-start.9
  67.6 2.6 %collective-permute-start.10 = (bf16[32,32,128]{2,1,0:T(8,128)(2,1)}, bf16[32,32,128]{2,1,0:T(8,128)(2,1)S(1)}, u32[]{:S(2)}, u32[]{:S(2)}) collective-permute-start(bf16[32,32,128]{2,1,0:T(8,128)(2,1)} %get-tuple-element.52), channel_id=1, source_target_pairs={{0,4},{1,5},{2,6},{3,7},{4,0},{5,1},{6,2},{7,3},{8,12},{9,13},{10,... | collective-permute-start | bytes 786440 | tf_op jit(solution)/shard_map/ppermute | solution.py:403
  70.3 2.4 %collective-permute-done.6.refs_6_ = bf16[32,32,128]{2,1,0:T(8,128)(2,1)S(1)} collective-permute-done((bf16[32,32,128]{2,1,0:T(8,128)(2,1)}, bf16[32,32,128]{2,1,0:T(8,128)(2,1)S(1)}, u32[]{:S(2)}, u32[]{:S(2)}) %collective-permute-start.6) | collective-permute-done | bytes 262176 | tf_op jit(solution)/shard_map/ppermute | solution.py:403
  72.7 0.5 collective-permute-start.11
  73.2 1.0 collective-permute-start.12
  74.1 0.8 collective-permute-start.13
  74.9 3.4 %collective-permute-done.9.refs_9_ = bf16[32,32,128]{2,1,0:T(8,128)(2,1)S(1)} collective-permute-done((bf16[32,32,128]{2,1,0:T(8,128)(2,1)}, bf16[32,32,128]{2,1,0:T(8,128)(2,1)S(1)}, u32[]{:S(2)}, u32[]{:S(2)}) %collective-permute-start.9) | collective-permute-done | bytes 262176 | tf_op jit(solution)/shard_map/ppermute | solution.py:403
  78.3 0.1 collective-permute-start.14
  78.4 5.6 %collective-permute-done.10.refs_10_ = bf16[32,32,128]{2,1,0:T(8,128)(2,1)S(1)} collective-permute-done((bf16[32,32,128]{2,1,0:T(8,128)(2,1)}, bf16[32,32,128]{2,1,0:T(8,128)(2,1)S(1)}, u32[]{:S(2)}, u32[]{:S(2)}) %collective-permute-start.10) | collective-permute-done | bytes 262176 | tf_op jit(solution)/shard_map/ppermute | solution.py:403
  84.0 2.8 %collective-permute-done.12.refs_12_ = bf16[32,32,128]{2,1,0:T(8,128)(2,1)S(1)} collective-permute-done((bf16[32,32,128]{2,1,0:T(8,128)(2,1)}, bf16[32,32,128]{2,1,0:T(8,128)(2,1)S(1)}, u32[]{:S(2)}, u32[]{:S(2)}) %collective-permute-start.12) | collective-permute-done | bytes 262176 | tf_op jit(solution)/shard_map/ppermute | solution.py:403
  86.8 6.6 %collective-permute-done.13.refs_13_ = bf16[32,32,128]{2,1,0:T(8,128)(2,1)S(1)} collective-permute-done((bf16[32,32,128]{2,1,0:T(8,128)(2,1)}, bf16[32,32,128]{2,1,0:T(8,128)(2,1)S(1)}, u32[]{:S(2)}, u32[]{:S(2)}) %collective-permute-start.13) | collective-permute-done | bytes 262176 | tf_op jit(solution)/shard_map/ppermute | solution.py:403
  93.5 0.6 copy-done.16
  94.0 0.1 copy-done.17
  94.2 0.9 copy-done.1
  95.1 9.9 %join_first.1 = (bf16[48,32,2112]{2,1,0:T(8,128)(2,1)}, f32[48,1,2112]{2,1,0:T(1,128)}, s32[35]{0:T(128)S(1)}) custom-call(s32[1]{0:T(128)} %bitcast.me_ref, s32[16,1,28]{2,1,0:T(1,128)} %bitcast.15, s32[16]{0:T(128)S(1)} %get-tuple-element.38.inner_ref, bf16[32,32,128]{2,1,0:T(8,128)(2,1)} %copy-done.3, bf16[32,32,128]{2,1,0:T(8,128)(2,1)} %copy-done.4, ...), custom_call_target="tpu_custom_call" | custom-call | flops 4000000000 | bytes 10000000 | tf_op jit(solution)/shard_map/join_first/pallas_call | solution.py:504
  105.0 1.9 %join_last.1 = (bf16[48,32,2112]{2,1,0:T(8,128)(2,1)}, f32[48,1,2112]{2,1,0:T(1,128)}) custom-call(s32[35]{0:T(128)S(1)} %get-tuple-element.58.late_ref, bf16[16,10,32,128]{3,2,1,0:T(8,128)(2,1)S(1)} %all-to-all-done.1.second_hbm, bf16[16,24,32,128]{3,2,1,0:T(8,128)(2,1)} %get-tuple-element.71.third_hbm, ...), custom_call_target="tpu_custom_call", output_to_operand_aliasing={{0}: (3, {}), {1}: (4, {})} | custom-call | flops 1000000000 | bytes 10000000 | tf_op jit(solution)/shard_map/join_last/pallas_call | solution.py:526
  (44 shorter events, 0.1 us)
Async XLA Ops:
  0.6 24.7 %copy-start = (s32[16,9]{1,0:T(8,128)S(1)}, s32[16,9]{1,0:T(8,128)}, u32[]{:S(2)}) copy-start(s32[16,9]{1,0:T(8,128)} %offset_ref.1) | copy-start | bytes 1732
  9.1 15.3 %collective-permute-start.15 = (bf16[17,32,128]{2,1,0:T(8,128)(2,1)S(1)}, bf16[17,32,128]{2,1,0:T(8,128)(2,1)S(1)}, u32[]{:S(2)}, u32[]{:S(2)}) collective-permute-start(bf16[17,32,128]{2,1,0:T(8,128)(2,1)S(1)} %get-tuple-element.60), channel_id=1, source_target_pairs={{0,16},{16,32},{32,48},{48,64},{64,80},{80,96},{96,112},{1,17},{17... | collective-permute-start | bytes 417800 | tf_op jit(solution)/shard_map/ppermute | solution.py:471
  14.1 11.3 %collective-permute-start.16 = (bf16[17,32,128]{2,1,0:T(8,128)(2,1)S(1)}, bf16[17,32,128]{2,1,0:T(8,128)(2,1)S(1)}, u32[]{:S(2)}, u32[]{:S(2)}) collective-permute-start(bf16[17,32,128]{2,1,0:T(8,128)(2,1)S(1)} %get-tuple-element.61), channel_id=1, source_target_pairs={{16,0},{32,16},{48,32},{64,48},{80,64},{96,80},{112,96},{17,1},{33... | collective-permute-start | bytes 417800 | tf_op jit(solution)/shard_map/ppermute | solution.py:472
  17.4 24.1 %collective-permute-start = (bf16[32,32,128]{2,1,0:T(8,128)(2,1)}, bf16[32,32,128]{2,1,0:T(8,128)(2,1)S(1)}, u32[]{:S(2)}, u32[]{:S(2)}) collective-permute-start(bf16[32,32,128]{2,1,0:T(8,128)(2,1)} %get-tuple-element.39), channel_id=1, source_target_pairs={{0,13},{1,12},{2,15},{3,14},{4,9},{5,8},{6,11},{7,10},{8,5},{9,4},... | collective-permute-start | bytes 786440 | tf_op jit(solution)/shard_map/ppermute | solution.py:403
  20.5 23.4 %collective-permute-start.1 = (bf16[32,32,128]{2,1,0:T(8,128)(2,1)}, bf16[32,32,128]{2,1,0:T(8,128)(2,1)S(1)}, u32[]{:S(2)}, u32[]{:S(2)}) collective-permute-start(bf16[32,32,128]{2,1,0:T(8,128)(2,1)} %get-tuple-element.40), channel_id=1, source_target_pairs={{0,12},{1,13},{2,14},{3,15},{4,8},{5,9},{6,10},{7,11},{8,4},{9,5},... | collective-permute-start | bytes 786440 | tf_op jit(solution)/shard_map/ppermute | solution.py:403
  21.7 23.4 %collective-permute-start.2 = (bf16[32,32,128]{2,1,0:T(8,128)(2,1)}, bf16[32,32,128]{2,1,0:T(8,128)(2,1)S(1)}, u32[]{:S(2)}, u32[]{:S(2)}) collective-permute-start(bf16[32,32,128]{2,1,0:T(8,128)(2,1)} %get-tuple-element.41), channel_id=1, source_target_pairs={{0,11},{1,10},{2,13},{3,12},{4,15},{5,14},{6,9},{7,8},{8,3},{9,2},... | collective-permute-start | bytes 786440 | tf_op jit(solution)/shard_map/ppermute | solution.py:403
  24.4 22.7 %collective-permute-start.3 = (bf16[32,32,128]{2,1,0:T(8,128)(2,1)}, bf16[32,32,128]{2,1,0:T(8,128)(2,1)S(1)}, u32[]{:S(2)}, u32[]{:S(2)}) collective-permute-start(bf16[32,32,128]{2,1,0:T(8,128)(2,1)} %get-tuple-element.42), channel_id=1, source_target_pairs={{0,7},{1,6},{2,1},{3,0},{4,3},{5,2},{6,5},{7,4},{8,15},{9,14},{10,... | collective-permute-start | bytes 786440 | tf_op jit(solution)/shard_map/ppermute | solution.py:403
  30.3 74.7 %all-to-all-start.1 = ((bf16[16,10,32,128]{3,2,1,0:T(8,128)(2,1)}), bf16[16,10,32,128]{3,2,1,0:T(8,128)(2,1)S(1)}, u32[]{:S(2)}, u32[]{:S(2)}) async-start(bf16[16,10,32,128]{3,2,1,0:T(8,128)(2,1)} %get-tuple-element.62), calls=%async_computation.1 | async-start | bytes 2621440 | tf_op jit(solution)/shard_map/all_to_all | solution.py:494
  39.8 27.2 %collective-permute-start.4 = (bf16[32,32,128]{2,1,0:T(8,128)(2,1)}, bf16[32,32,128]{2,1,0:T(8,128)(2,1)S(1)}, u32[]{:S(2)}, u32[]{:S(2)}) collective-permute-start(bf16[32,32,128]{2,1,0:T(8,128)(2,1)} %get-tuple-element.46), channel_id=1, source_target_pairs={{0,3},{1,2},{2,5},{3,4},{4,7},{5,6},{6,1},{7,0},{8,11},{9,10},{10,... | collective-permute-start | bytes 786440 | tf_op jit(solution)/shard_map/ppermute | solution.py:403
  41.5 51.8 %copy-start.3 = (bf16[32,32,128]{2,1,0:T(8,128)(2,1)}, bf16[32,32,128]{2,1,0:T(8,128)(2,1)S(1)}, u32[]{:S(2)}) copy-start(bf16[32,32,128]{2,1,0:T(8,128)(2,1)S(1)} %collective-permute-done.refs_0_) | copy-start | bytes 786436
  41.5 26.1 %collective-permute-start.5 = (bf16[32,32,128]{2,1,0:T(8,128)(2,1)}, bf16[32,32,128]{2,1,0:T(8,128)(2,1)S(1)}, u32[]{:S(2)}, u32[]{:S(2)}) collective-permute-start(bf16[32,32,128]{2,1,0:T(8,128)(2,1)} %get-tuple-element.47), channel_id=1, source_target_pairs={{0,10},{1,11},{2,12},{3,13},{4,14},{5,15},{6,8},{7,9},{8,2},{9,3},... | collective-permute-start | bytes 786440 | tf_op jit(solution)/shard_map/ppermute | solution.py:403
  43.9 49.4 %copy-start.4 = (bf16[32,32,128]{2,1,0:T(8,128)(2,1)}, bf16[32,32,128]{2,1,0:T(8,128)(2,1)S(1)}, u32[]{:S(2)}) copy-start(bf16[32,32,128]{2,1,0:T(8,128)(2,1)S(1)} %collective-permute-done.1.refs_1_) | copy-start | bytes 786436
  43.9 28.8 %collective-permute-start.6 = (bf16[32,32,128]{2,1,0:T(8,128)(2,1)}, bf16[32,32,128]{2,1,0:T(8,128)(2,1)S(1)}, u32[]{:S(2)}, u32[]{:S(2)}) collective-permute-start(bf16[32,32,128]{2,1,0:T(8,128)(2,1)} %get-tuple-element.48), channel_id=1, source_target_pairs={{0,2},{1,3},{2,4},{3,5},{4,6},{5,7},{6,0},{7,1},{8,10},{9,11},{10,... | collective-permute-start | bytes 786440 | tf_op jit(solution)/shard_map/ppermute | solution.py:403
  45.1 48.3 %copy-start.5 = (bf16[32,32,128]{2,1,0:T(8,128)(2,1)}, bf16[32,32,128]{2,1,0:T(8,128)(2,1)S(1)}, u32[]{:S(2)}) copy-start(bf16[32,32,128]{2,1,0:T(8,128)(2,1)S(1)} %collective-permute-done.2.refs_2_) | copy-start | bytes 786436
  45.1 28.1 %collective-permute-start.7 = (bf16[32,32,128]{2,1,0:T(8,128)(2,1)}, bf16[32,32,128]{2,1,0:T(8,128)(2,1)S(1)}, u32[]{:S(2)}, u32[]{:S(2)}) collective-permute-start(bf16[32,32,128]{2,1,0:T(8,128)(2,1)} %get-tuple-element.49), channel_id=1, source_target_pairs={{0,6},{1,7},{2,0},{3,1},{4,2},{5,3},{6,4},{7,5},{8,14},{9,15},{10,... | collective-permute-start | bytes 786440 | tf_op jit(solution)/shard_map/ppermute | solution.py:403
  47.1 46.2 %copy-start.6 = (bf16[32,32,128]{2,1,0:T(8,128)(2,1)}, bf16[32,32,128]{2,1,0:T(8,128)(2,1)S(1)}, u32[]{:S(2)}) copy-start(bf16[32,32,128]{2,1,0:T(8,128)(2,1)S(1)} %collective-permute-done.3.refs_3_) | copy-start | bytes 786436
  47.2 27.0 %collective-permute-start.8 = (bf16[32,32,128]{2,1,0:T(8,128)(2,1)}, bf16[32,32,128]{2,1,0:T(8,128)(2,1)S(1)}, u32[]{:S(2)}, u32[]{:S(2)}) collective-permute-start(bf16[32,32,128]{2,1,0:T(8,128)(2,1)} %get-tuple-element.50), channel_id=1, source_target_pairs={{0,15},{1,14},{2,9},{3,8},{4,11},{5,10},{6,13},{7,12},{8,7},{9,6},... | collective-permute-start | bytes 786440 | tf_op jit(solution)/shard_map/ppermute | solution.py:403
  67.0 26.4 %copy-start.7 = (bf16[32,32,128]{2,1,0:T(8,128)(2,1)}, bf16[32,32,128]{2,1,0:T(8,128)(2,1)S(1)}, u32[]{:S(2)}) copy-start(bf16[32,32,128]{2,1,0:T(8,128)(2,1)S(1)} %collective-permute-done.4.refs_4_) | copy-start | bytes 786436
  67.0 11.3 %collective-permute-start.9 = (bf16[32,32,128]{2,1,0:T(8,128)(2,1)}, bf16[32,32,128]{2,1,0:T(8,128)(2,1)S(1)}, u32[]{:S(2)}, u32[]{:S(2)}) collective-permute-start(bf16[32,32,128]{2,1,0:T(8,128)(2,1)} %get-tuple-element.51), channel_id=1, source_target_pairs={{0,5},{1,4},{2,7},{3,6},{4,1},{5,0},{6,3},{7,2},{8,13},{9,12},{10,... | collective-permute-start | bytes 786440 | tf_op jit(solution)/shard_map/ppermute | solution.py:403
  67.6 25.8 %copy-start.8 = (bf16[32,32,128]{2,1,0:T(8,128)(2,1)}, bf16[32,32,128]{2,1,0:T(8,128)(2,1)S(1)}, u32[]{:S(2)}) copy-start(bf16[32,32,128]{2,1,0:T(8,128)(2,1)S(1)} %collective-permute-done.5.refs_5_) | copy-start | bytes 786436
  67.6 16.3 %collective-permute-start.10 = (bf16[32,32,128]{2,1,0:T(8,128)(2,1)}, bf16[32,32,128]{2,1,0:T(8,128)(2,1)S(1)}, u32[]{:S(2)}, u32[]{:S(2)}) collective-permute-start(bf16[32,32,128]{2,1,0:T(8,128)(2,1)} %get-tuple-element.52), channel_id=1, source_target_pairs={{0,4},{1,5},{2,6},{3,7},{4,0},{5,1},{6,2},{7,3},{8,12},{9,13},{10,... | collective-permute-start | bytes 786440 | tf_op jit(solution)/shard_map/ppermute | solution.py:403
  72.7 20.7 %copy-start.9 = (bf16[32,32,128]{2,1,0:T(8,128)(2,1)}, bf16[32,32,128]{2,1,0:T(8,128)(2,1)S(1)}, u32[]{:S(2)}) copy-start(bf16[32,32,128]{2,1,0:T(8,128)(2,1)S(1)} %collective-permute-done.6.refs_6_) | copy-start | bytes 786436
  72.7 11.3 %collective-permute-start.11 = (bf16[32,32,128]{2,1,0:T(8,128)(2,1)}, bf16[32,32,128]{2,1,0:T(8,128)(2,1)S(1)}, u32[]{:S(2)}, u32[]{:S(2)}) collective-permute-start(bf16[32,32,128]{2,1,0:T(8,128)(2,1)} %get-tuple-element.53), channel_id=1, source_target_pairs={{0,14},{1,15},{2,8},{3,9},{4,10},{5,11},{6,12},{7,13},{8,6},{9,7},... | collective-permute-start | bytes 786440 | tf_op jit(solution)/shard_map/ppermute | solution.py:403
  73.2 20.2 %copy-start.10 = (bf16[32,32,128]{2,1,0:T(8,128)(2,1)}, bf16[32,32,128]{2,1,0:T(8,128)(2,1)S(1)}, u32[]{:S(2)}) copy-start(bf16[32,32,128]{2,1,0:T(8,128)(2,1)S(1)} %collective-permute-done.7.refs_7_) | copy-start | bytes 786436
  73.2 13.6 %collective-permute-start.12 = (bf16[32,32,128]{2,1,0:T(8,128)(2,1)}, bf16[32,32,128]{2,1,0:T(8,128)(2,1)S(1)}, u32[]{:S(2)}, u32[]{:S(2)}) collective-permute-start(bf16[32,32,128]{2,1,0:T(8,128)(2,1)} %get-tuple-element.54), channel_id=1, source_target_pairs={{0,9},{1,8},{2,11},{3,10},{4,13},{5,12},{6,15},{7,14},{8,1},{9,0},... | collective-permute-start | bytes 786440 | tf_op jit(solution)/shard_map/ppermute | solution.py:403
  74.1 19.3 %copy-start.11 = (bf16[32,32,128]{2,1,0:T(8,128)(2,1)}, bf16[32,32,128]{2,1,0:T(8,128)(2,1)S(1)}, u32[]{:S(2)}) copy-start(bf16[32,32,128]{2,1,0:T(8,128)(2,1)S(1)} %collective-permute-done.8.refs_8_) | copy-start | bytes 786436
  74.1 19.2 %collective-permute-start.13 = (bf16[32,32,128]{2,1,0:T(8,128)(2,1)}, bf16[32,32,128]{2,1,0:T(8,128)(2,1)S(1)}, u32[]{:S(2)}, u32[]{:S(2)}) collective-permute-start(bf16[32,32,128]{2,1,0:T(8,128)(2,1)} %get-tuple-element.55), channel_id=1, source_target_pairs={{0,8},{1,9},{2,10},{3,11},{4,12},{5,13},{6,14},{7,15},{8,0},{9,1},... | collective-permute-start | bytes 786440 | tf_op jit(solution)/shard_map/ppermute | solution.py:403
  78.3 15.2 %copy-start.12 = (bf16[32,32,128]{2,1,0:T(8,128)(2,1)}, bf16[32,32,128]{2,1,0:T(8,128)(2,1)S(1)}, u32[]{:S(2)}) copy-start(bf16[32,32,128]{2,1,0:T(8,128)(2,1)S(1)} %collective-permute-done.9.refs_9_) | copy-start | bytes 786436
  78.3 15.1 %collective-permute-start.14 = (bf16[32,32,128]{2,1,0:T(8,128)(2,1)}, bf16[32,32,128]{2,1,0:T(8,128)(2,1)S(1)}, u32[]{:S(2)}, u32[]{:S(2)}) collective-permute-start(bf16[32,32,128]{2,1,0:T(8,128)(2,1)} %get-tuple-element.56), channel_id=1, source_target_pairs={{0,1},{1,0},{2,3},{3,2},{4,5},{5,4},{6,7},{7,6},{8,9},{9,8},{10,11... | collective-permute-start | bytes 786440 | tf_op jit(solution)/shard_map/ppermute | solution.py:403
  83.9 9.5 %copy-start.13 = (bf16[32,32,128]{2,1,0:T(8,128)(2,1)}, bf16[32,32,128]{2,1,0:T(8,128)(2,1)S(1)}, u32[]{:S(2)}) copy-start(bf16[32,32,128]{2,1,0:T(8,128)(2,1)S(1)} %collective-permute-done.10.refs_10_) | copy-start | bytes 786436
  83.9 9.5 %copy-start.14 = (bf16[32,32,128]{2,1,0:T(8,128)(2,1)}, bf16[32,32,128]{2,1,0:T(8,128)(2,1)S(1)}, u32[]{:S(2)}) copy-start(bf16[32,32,128]{2,1,0:T(8,128)(2,1)S(1)} %collective-permute-done.11.refs_11_) | copy-start | bytes 786436
  86.8 6.7 %copy-start.15 = (bf16[32,32,128]{2,1,0:T(8,128)(2,1)}, bf16[32,32,128]{2,1,0:T(8,128)(2,1)S(1)}, u32[]{:S(2)}) copy-start(bf16[32,32,128]{2,1,0:T(8,128)(2,1)S(1)} %collective-permute-done.12.refs_12_) | copy-start | bytes 786436
  (3 other events, 2.5 us)
